TPU v7x, 32 devices: a whole 2x2x4 slice. The times are simulated.
32 devices in a mesh: grp: 16 (over z, y, x), rep: 2 (over core).
Axes of the slice: x: 2, y: 2, z: 4, core: 2. Of those that a mesh axis runs over, the one named last changes fastest.
Arguments:
- snapshots: float32 [16, 2048, 1024], P('grp', 'rep'), may hold values from -6 to 6
- row_factor: float32 [2048, 128], P('rep'), may hold values from -0.125 to 0.125
- time_factor: float32 [16, 8], replicated, may hold values from -1.5 to 1.5
Outputs:
- new_rows: float32 [2048, 128], P('rep')
- new_time: float32 [16, 8], replicated
All inputs are finite; a program needn't handle non-finite values.
Results may differ from a plain program's by a relative error of at most 0.0001.
Values sent between devices are 32-bit elements; how exact they have to be, the bound alone decides.
No kernel may reach another device: no remote copies, remote signals or barrier semaphores. Data moves between devices by JAX's collectives and lax.ppermute only.
A program may use at most 64 MiB of HBM per device.

v0:
```python
import math

import jax
import jax.numpy as jnp
from jax import lax
from jax.sharding import PartitionSpec as P

STEPS = 8
HIGHEST = lax.Precision.HIGHEST
HIGH = lax.Precision.HIGH


def highdot(left, right):
    return jnp.dot(left, right, precision=HIGHEST, preferred_element_type=jnp.float32)


def orthogonalize(start_matrix):
    total = jnp.sum(start_matrix * start_matrix)
    iterate = start_matrix / jnp.sqrt(total + 1e-06)
    for step_index in range(STEPS):
        inner = highdot(iterate.T, iterate)
        iterate = 1.5 * iterate - 0.5 * highdot(iterate, inner)
    return iterate


def orth_factor(gram):
    rank = gram.shape[0]
    eye = jnp.eye(rank, dtype=jnp.float32)
    total = jnp.sum(gram * eye) + 1e-06
    squared = gram / total
    factor = eye / jnp.sqrt(total)
    for step_index in range(STEPS):
        turn = 1.5 * eye - 0.5 * squared
        factor = highdot(factor, turn)
        if step_index < STEPS - 1:
            squared = highdot(highdot(squared, turn), turn)
    return factor


def sum_of_small(part, axes, devices):
    if devices * part.size > 1 << 20:
        return lax.psum(part, axes)
    copies = jnp.broadcast_to(part.reshape(1, -1), (devices, part.size))
    received = lax.all_to_all(copies, axes, split_axis=0, concat_axis=0, tiled=True)
    return jnp.sum(received, axis=0).reshape(part.shape)


def make_on_device(groups_n, reps):
    half_n = groups_n // 2
    halves = [[h * half_n + i for i in range(half_n)] for h in range(2)]
    across = [(i, (i + half_n) % groups_n) for i in range(groups_n)]
    swap = [(0, 1), (1, 0)]

    def on_device(snapshots, row_factor, time_factor):
        rows, cols = snapshots.shape[1:]
        rank = row_factor.shape[1]
        width = cols // reps
        me = lax.axis_index("rep")
        image = snapshots[0]
        projected = jnp.einsum("ij,ia->aj", image, row_factor, precision=HIGH, preferred_element_type=jnp.float32)
        keep = lax.dynamic_slice_in_dim(projected, me * width, width, 1)
        send = lax.dynamic_slice_in_dim(projected, (1 - me) * width, width, 1)
        summed = keep + lax.ppermute(send, "rep", swap)
        owned = lax.all_to_all(
            summed.reshape(groups_n, rank // groups_n, width), "grp", split_axis=0, concat_axis=0, tiled=True
        )
        flat = owned.reshape(groups_n, -1)
        gram_total = sum_of_small(highdot(flat, flat.T), ("grp", "rep"), groups_n * reps)
        basis_time = orthogonalize(highdot(gram_total, time_factor))
        mixer = highdot(basis_time, basis_time.T)
        weights = highdot(mixer, flat).reshape(owned.shape)
        mine = lax.all_to_all(weights, "grp", split_axis=0, concat_axis=0, tiled=True).reshape(rank, width)
        other = lax.ppermute(mine, "rep", swap)
        left = jnp.where(me == 0, mine, other)
        right = jnp.where(me == 0, other, mine)
        full = jnp.concatenate([left, right], axis=1)
        product = jnp.einsum("ij,aj->ia", image, full, precision=HIGH, preferred_element_type=jnp.float32)
        parts = lax.all_to_all(
            product.reshape(half_n, rows // half_n, rank),
            "grp",
            split_axis=0,
            concat_axis=0,
            tiled=True,
            axis_index_groups=halves,
        )
        chunk = jnp.sum(parts, axis=0)
        chunk = chunk + lax.ppermute(chunk, "grp", across)
        block = lax.all_to_all(
            jnp.broadcast_to(chunk[None], (half_n,) + chunk.shape),
            "grp",
            split_axis=0,
            concat_axis=0,
            tiled=True,
            axis_index_groups=halves,
        ).reshape(rows, rank)
        gram = highdot(block.T, block)
        gram = gram + lax.ppermute(gram, "rep", swap)
        new_rows = highdot(block, orth_factor(gram) * math.sqrt(rows * reps))
        return (new_rows, basis_time * math.sqrt(groups_n))

    return on_device


def solution(mesh):
    return jax.shard_map(
        make_on_device(mesh.shape["grp"], mesh.shape["rep"]),
        mesh=mesh,
        in_specs=(P("grp", "rep", None), P("rep", None), P()),
        out_specs=(P("rep", None), P()),
        check_vma=False,
    )
```

profile of v0, /device:TPU:0, one launch (start us, length us, event | category | flops | bytes accessed | tf_op | source)
XLA Modules:
  0.0 98.9 jit_solution(2043464388775029604)
XLA Ops:
  0.7 1.0 %copy-done = f32[1024,128]{1,0:T(8,128)S(1)} copy-done((f32[1024,128]{1,0:T(8,128)S(1)}, f32[1024,128]{1,0:T(8,128)}, u32[]{:S(2)}) %copy-start) | copy-done | bytes 524312
  1.7 3.5 %fusion.2 = f32[128,1024]{1,0:T(8,128)S(1)} fusion(f32[1024,128]{1,0:T(8,128)S(1)} %copy-done, f32[1,1024,1024]{2,1,0:T(8,128)} %param.3), kind=kOutput, calls=%fused_computation.2 | convolution fusion | flops 805306368 | bytes 5242880 | tf_op jit(solution)/shard_map/ij,ia->aj/dot_general | solution.py:60
  5.2 0.6 collective-permute-start
  5.7 1.2 %collective-permute-done = f32[128,512]{1,0:T(8,128)S(1)} collective-permute-done((f32[128,512]{1,0:T(8,128)S(1)}, f32[128,512]{1,0:T(8,128)S(1)}, u32[]{:S(2)}, u32[]{:S(2)}) %collective-permute-start) | collective-permute-done | bytes 262176 | tf_op jit(solution)/shard_map/ppermute | solution.py:63
  7.0 18.2 %all_to_all.26 = f32[16,8,512]{2,1,0:T(8,128)S(1)} all-to-all(f32[16,8,512]{2,1,0:T(8,128)S(1)} %add_bitcast_fusion), channel_id=1, replica_groups=mesh['grp'=16,'rep'=2] {'grp'}, dimensions={0} | all-to-all | bytes 524288 | tf_op jit(solution)/shard_map/all_to_all | solution.py:64
  25.1 0.5 convolution_bitcast_fusion.2
  25.7 0.1 broadcast_in_dim.6
  25.8 9.6 %all_to_all.27 = f32[32,1,256]{2,1,0:T(1,128)S(1)} all-to-all(f32[32,1,256]{2,1,0:T(1,128)S(1)} %broadcast_in_dim.14), channel_id=1, replica_groups=mesh['grp'=16,'rep'=2] {'grp','rep'}, dimensions={0} | all-to-all | bytes 65536 | tf_op jit(solution)/shard_map/all_to_all | solution.py:44
  35.5 0.1 reshape.35
  35.5 0.7 multiply_reduce_fusion
  37.0 0.1 fusion.108
  37.1 0.2 fusion.15
  37.3 0.1 fusion.173
  37.4 0.2 fusion.14
  37.6 0.1 fusion.174
  37.8 0.2 fusion.13
  38.0 0.1 fusion.175
  38.1 0.2 fusion.12
  38.3 0.1 fusion.176
  38.5 0.2 fusion.11
  38.7 0.1 fusion.177
  38.8 0.2 fusion.10
  39.0 0.1 fusion.178
  39.2 0.2 fusion.9
  39.4 0.1 fusion.179
  39.5 0.8 broadcast_multiply_fusion
  40.3 0.2 convolution_bitcast_fusion.1
  40.5 0.5 fusion.19
  41.0 0.2 copy.32
  41.2 13.0 %all_to_all.28 = f32[16,8,512]{2,1,0:T(8,128)S(1)} all-to-all(f32[16,8,512]{2,1,0:T(8,128)S(1)} %copy.32), channel_id=1, replica_groups=mesh['grp'=16,'rep'=2] {'grp'}, dimensions={0} | all-to-all | bytes 524288 | tf_op jit(solution)/shard_map/all_to_all | solution.py:72
  54.2 1.5 %collective-permute-done.1 = f32[128,512]{1,0:T(8,128)S(1)} collective-permute-done((f32[128,512]{1,0:T(8,128)S(1)}, f32[128,512]{1,0:T(8,128)S(1)}, u32[]{:S(2)}, u32[]{:S(2)}) %collective-permute-start.1) | collective-permute-done | bytes 262176 | tf_op jit(solution)/shard_map/ppermute | solution.py:73
  55.7 4.4 %fusion.4 = f32[16,8,8,128]{3,2,1,0:T(8,128)S(1)} fusion(f32[1,1024,1024]{2,1,0:T(8,128)} %param.3, f32[128,512]{1,0:T(8,128)S(1)} %get-tuple-element.5, f32[128,512]{1,0:T(8,128)S(1)} %get-tuple-element.4), kind=kOutput, calls=%fused_computation.4 | convolution fusion | flops 805437440 | bytes 5242880 | tf_op jit(solution)/shard_map/ij,aj->ia/dot_general | solution.py:77
  60.2 12.4 %all_to_all.29 = f32[8,128,128]{1,2,0:T(8,128)S(1)} all-to-all(f32[8,128,128]{1,2,0:T(8,128)S(1)} %bitcast.98), channel_id=1, replica_groups={{0,2,4,6,8,10,12,14},{16,18,20,22,24,26,28,30},{1,3,5,7,9,11,13,15},{17..., dimensions={0} | all-to-all | bytes 1048576 | tf_op jit(solution)/shard_map/all_to_all | solution.py:78
  72.6 1.1 %collective-permute-start.2 = (f32[128,128]{0,1:T(8,128)S(1)}, f32[128,128]{0,1:T(8,128)S(1)}, u32[]{:S(2)}, u32[]{:S(2)}) collective-permute-start(f32[128,128]{0,1:T(8,128)S(1)} %reduce_sum.38), channel_id=1, source_target_pairs={{0,16},{2,18},{4,20},{6,22},{8,24},{10,26},{12,28},{14,30},{16,0},... | collective-permute-start | bytes 196616 | tf_op jit(solution)/shard_map/ppermute | solution.py:87
  73.8 4.8 %collective-permute-done.2 = f32[128,128]{0,1:T(8,128)S(1)} collective-permute-done((f32[128,128]{0,1:T(8,128)S(1)}, f32[128,128]{0,1:T(8,128)S(1)}, u32[]{:S(2)}, u32[]{:S(2)}) %collective-permute-start.2) | collective-permute-done | bytes 65568 | tf_op jit(solution)/shard_map/ppermute | solution.py:87
  78.6 0.1 copy.35
  78.7 10.4 %all_to_all.30 = f32[8,128,128]{2,1,0:T(8,128)S(1)} all-to-all(f32[8,128,128]{2,1,0:T(8,128)S(1)} %broadcast_in_dim.15), channel_id=1, replica_groups={{0,2,4,6,8,10,12,14},{16,18,20,22,24,26,28,30},{1,3,5,7,9,11,13,15},{17..., dimensions={0} | all-to-all | bytes 1048576 | tf_op jit(solution)/shard_map/all_to_all | solution.py:88
  89.2 1.0 %convolution_bitcast_fusion = f32[128,128]{1,0:T(8,128)S(1)} fusion(f32[8,128,128]{2,1,0:T(8,128)S(1)} %all_to_all.30), kind=kOutput, calls=%fused_computation.8 | convolution fusion | flops 201326592 | bytes 589824 | tf_op jit(solution)/shard_map/dot_general | solution.py:14
  90.2 0.1 collective-permute-start.3
  90.3 1.2 %collective-permute-done.3 = f32[128,128]{1,0:T(8,128)S(1)} collective-permute-done((f32[128,128]{1,0:T(8,128)S(1)}, f32[128,128]{1,0:T(8,128)S(1)}, u32[]{:S(2)}, u32[]{:S(2)}) %collective-permute-start.3) | collective-permute-done | bytes 65568 | tf_op jit(solution)/shard_map/ppermute | solution.py:97
  91.5 0.6 select_reduce_fusion
  92.8 0.2 fusion.28
  93.0 0.2 fusion.25
  93.3 0.2 fusion.27
  93.5 0.2 fusion.30
  93.7 0.2 fusion.31
  93.9 0.2 fusion.29
  94.1 0.2 fusion.33
  94.3 0.2 fusion.34
  94.5 0.2 fusion.32
  94.8 0.2 fusion.36
  95.0 0.2 fusion.37
  95.2 0.2 fusion.35
  95.4 0.2 fusion.39
  95.6 0.2 fusion.40
  95.8 0.2 fusion.38
  96.1 0.2 fusion.42
  96.3 0.2 fusion.43
  96.5 0.2 fusion.41
  96.7 0.2 fusion.23
  96.9 0.2 fusion.24
  97.1 0.2 fusion.7
  97.3 0.2 convolution_multiply_fusion
  97.6 1.4 %fusion.180 = f32[1024,128]{1,0:T(8,128)} fusion(f32[1024,128]{1,0:T(8,128)S(1)} %bitcast.96, f32[128,128]{1,0:T(8,128)S(1)} %convolution_multiply_fusion), kind=kOutput, calls=%fused_computation.210 | convolution fusion | flops 201326592 | bytes 1114112 | tf_op jit(solution)/shard_map/dot_general | solution.py:14
  (13 shorter events, 0.3 us)
Async XLA Ops:
  0.6 1.0 %copy-start = (f32[1024,128]{1,0:T(8,128)S(1)}, f32[1024,128]{1,0:T(8,128)}, u32[]{:S(2)}) copy-start(f32[1024,128]{1,0:T(8,128)} %param.4) | copy-start | bytes 1572868
  0.6 34.9 %copy-start.1 = (f32[16,8]{0,1:T(8,128)S(1)}, f32[16,8]{0,1:T(8,128)}, u32[]{:S(2)}) copy-start(f32[16,8]{0,1:T(8,128)} %param.5) | copy-start | bytes 1540
  5.2 1.7 %collective-permute-start = (f32[128,512]{1,0:T(8,128)S(1)}, f32[128,512]{1,0:T(8,128)S(1)}, u32[]{:S(2)}, u32[]{:S(2)}) collective-permute-start(f32[128,512]{1,0:T(8,128)S(1)} %constant_dynamic-slice_fusion), channel_id=1, source_target_pairs={{0,1},{1,0},{2,3},{3,2},{4,5},{5,4},{6,7},{7,6},{8,9},{9,8},{10,11... | collective-permute-start | bytes 786440 | tf_op jit(solution)/shard_map/ppermute | solution.py:63
  54.2 1.5 %collective-permute-start.1 = (f32[128,512]{1,0:T(8,128)S(1)}, f32[128,512]{1,0:T(8,128)S(1)}, u32[]{:S(2)}, u32[]{:S(2)}) collective-permute-start(f32[128,512]{1,0:T(8,128)S(1)} %bitcast.99), channel_id=1, source_target_pairs={{0,1},{1,0},{2,3},{3,2},{4,5},{5,4},{6,7},{7,6},{8,9},{9,8},{10,11... | collective-permute-start | bytes 786440 | tf_op jit(solution)/shard_map/ppermute | solution.py:73
  72.6 5.9 %collective-permute-start.2 = (f32[128,128]{0,1:T(8,128)S(1)}, f32[128,128]{0,1:T(8,128)S(1)}, u32[]{:S(2)}, u32[]{:S(2)}) collective-permute-start(f32[128,128]{0,1:T(8,128)S(1)} %reduce_sum.38), channel_id=1, source_target_pairs={{0,16},{2,18},{4,20},{6,22},{8,24},{10,26},{12,28},{14,30},{16,0},... | collective-permute-start | bytes 196616 | tf_op jit(solution)/shard_map/ppermute | solution.py:87
  90.2 1.3 %collective-permute-start.3 = (f32[128,128]{1,0:T(8,128)S(1)}, f32[128,128]{1,0:T(8,128)S(1)}, u32[]{:S(2)}, u32[]{:S(2)}) collective-permute-start(f32[128,128]{1,0:T(8,128)S(1)} %convolution_bitcast_fusion), channel_id=1, source_target_pairs={{0,1},{1,0},{2,3},{3,2},{4,5},{5,4},{6,7},{7,6},{8,9},{9,8},{10,11... | collective-permute-start | bytes 196616 | tf_op jit(solution)/shard_map/ppermute | solution.py:97
where the time goes:
time: 99.3 us; the launch traced here: 98.9 us
  blocking collectives  63.6 us (64%)
  matrix products  20.1 us (20%)
  waiting for transfers between devices  8.73 us (9%)
  between operations  2.33 us (2%)
  starting transfers between devices  1.77 us (2%)
  local copies, waits for them, and re-layouts  1.58 us (2%)
    all_to_all x1, blocking collectives, on_device(): lax.all_to_all(summed.reshape(groups_n, rank // groups_n, width), 'grp',...  18.2 us
    all_to_all x1, blocking collectives, on_device(): lax.all_to_all(weights, 'grp', split_axis=0, concat_axis=0, tiled=True)  13 us
    all_to_all x1, blocking collectives, on_device(): lax.all_to_all(product.reshape(half_n, rows // half_n, rank), 'grp', spli...  12.4 us
    dot_general x44, matrix products, highdot(): jnp.dot(left, right, precision=HIGHEST, preferred_element_type=jnp.float32)  12.2 us
    all_to_all x1, blocking collectives, on_device(): lax.all_to_all(jnp.broadcast_to(chunk[None], (half_n,) + chunk.shape), 'g...  10.4 us
    all_to_all x1, blocking collectives, sum_of_small(): lax.all_to_all(copies, axes, split_axis=0, concat_axis=0, tiled=True)  9.59 us
    ppermute x1, waiting for transfers between devices, on_device(): chunk = chunk + lax.ppermute(chunk, 'grp', across)  4.8 us
    dot_general x1, matrix products, on_device(): jnp.einsum('ij,aj->ia', image, full, precision=HIGH, preferred_element_ty...  4.41 us
  transfers between devices with their start and end apart: 4, of which 4 were waited for; matrix products, arithmetic and copies ran while one was open for 0% of the time, Pallas kernels for 0%

commit v1 on v0

v1 whole, which is shorter than its diff:
```python
import functools
import math

import jax
import jax.numpy as jnp
from jax import lax
from jax.experimental import pallas as pl
from jax.experimental.pallas import tpu as pltpu
from jax.sharding import PartitionSpec as P

STEPS = 8
F32 = jnp.float32
BF16 = jnp.bfloat16
TINY = 1e-06


def dot(left, right, contract=((1,), (0,))):
    return lax.dot_general(
        left, right, (contract, ((), ())), precision=lax.Precision.HIGHEST, preferred_element_type=F32
    )


def fastdot(left, right, contract):
    return lax.dot_general(left, right, (contract, ((), ())), preferred_element_type=F32)


def split(value):
    high = value.astype(BF16)
    return high, (value - high.astype(F32)).astype(BF16)


def eye(size):
    return (lax.broadcasted_iota(jnp.int32, (size, size), 0) == lax.broadcasted_iota(jnp.int32, (size, size), 1)).astype(F32)


def orth_factor(gram):
    unit = eye(gram.shape[0])
    total = jnp.sum(gram * unit) + TINY
    squared = gram * (1.0 / total)
    factor = unit * lax.rsqrt(total)
    for step_index in range(STEPS):
        turn = 1.5 * unit - 0.5 * squared
        factor = dot(factor, turn)
        if step_index < STEPS - 1:
            squared = dot(dot(squared, turn), turn)
    return factor


def project_kernel(which_ref, image_ref, factor_ref, out_ref):
    image_high, image_low = split(image_ref[...])
    factor_high, factor_low = split(factor_ref[...])
    rank = factor_high.shape[1]
    both = jnp.concatenate([factor_high, factor_low], axis=1)
    wide = fastdot(both, image_high, ((0,), (0,)))
    value = wide[:rank] + wide[rank:] + fastdot(factor_high, image_low, ((0,), (0,)))

    @pl.when(pl.program_id(0) == 0)
    def _():
        out_ref[...] = value

    @pl.when(pl.program_id(0) > 0)
    def _():
        out_ref[...] += value


def project(image, row_factor, which, width, blocks=4):
    rows = image.shape[0]
    rank = row_factor.shape[1]
    block = rows // blocks
    return pl.pallas_call(
        project_kernel,
        grid_spec=pltpu.PrefetchScalarGridSpec(
            num_scalar_prefetch=1,
            grid=(blocks,),
            in_specs=[
                pl.BlockSpec((block, width), lambda i, which_ref: (i, which_ref[0])),
                pl.BlockSpec((block, rank), lambda i, which_ref: (i, 0)),
            ],
            out_specs=pl.BlockSpec((rank, width), lambda i, which_ref: (0, 0)),
        ),
        out_shape=jax.ShapeDtypeStruct((rank, width), F32),
        cost_estimate=pl.CostEstimate(
            flops=6 * rows * width * rank, bytes_accessed=4 * rows * (width + rank), transcendentals=0
        ),
        name="project",
    )(which, image, row_factor)


def product_kernel(which_ref, image_ref, weight_ref, *refs):
    out_ref = refs[-1]
    image_high, image_low = split(image_ref[...])
    weight_high, weight_low = split(weight_ref[...])
    rank = weight_high.shape[0]
    both = jnp.concatenate([weight_high, weight_low], axis=0)
    wide = fastdot(image_high, both, ((1,), (1,)))
    value = wide[:, :rank] + wide[:, rank:] + fastdot(image_low, weight_high, ((1,), (1,)))
    if len(refs) > 1:
        value = value + refs[0][...]
    out_ref[...] = value


def multiply(image, weight, which, start=None, blocks=4):
    rows = image.shape[0]
    rank, width = weight.shape
    block = rows // blocks
    out_spec = pl.BlockSpec((block, rank), lambda i, which_ref: (i, 0))
    more = [] if start is None else [start]
    return pl.pallas_call(
        product_kernel,
        grid_spec=pltpu.PrefetchScalarGridSpec(
            num_scalar_prefetch=1,
            grid=(blocks,),
            in_specs=[
                pl.BlockSpec((block, width), lambda i, which_ref: (i, which_ref[0])),
                pl.BlockSpec((rank, width), lambda i, which_ref: (0, 0)),
            ]
            + [out_spec for _ in more],
            out_specs=out_spec,
        ),
        out_shape=jax.ShapeDtypeStruct((rows, rank), F32),
        cost_estimate=pl.CostEstimate(
            flops=6 * rows * width * rank, bytes_accessed=4 * rows * (width + rank), transcendentals=0
        ),
        name="multiply",
    )(which, image, weight, *more)


def spread(groups_n, rank):
    rows = lax.broadcasted_iota(jnp.int32, (rank, groups_n), 0) // (rank // groups_n)
    return (rows == lax.broadcasted_iota(jnp.int32, (rank, groups_n), 1)).astype(F32)


def same_slot(groups_n, rank):
    per = rank // groups_n
    left = lax.broadcasted_iota(jnp.int32, (rank, rank), 0) % per
    right = lax.broadcasted_iota(jnp.int32, (rank, rank), 1) % per
    return left == right


def gram_kernel(owned_ref, out_ref):
    owned = owned_ref[...]
    groups_n = out_ref.shape[0]
    rank = owned.shape[0]
    full = jnp.where(same_slot(groups_n, rank), dot(owned, owned, ((1,), (1,))), 0.0)
    fold = spread(groups_n, rank)
    out_ref[...] = dot(dot(fold, full, ((0,), (0,))), fold)


def small_gram(owned, groups_n):
    return pl.pallas_call(
        gram_kernel, out_shape=jax.ShapeDtypeStruct((groups_n, groups_n), F32), name="small_gram"
    )(owned)


def mix_kernel(gram_ref, time_ref, owned_ref, out_ref, time_out_ref):
    groups_n = gram_ref.shape[0]
    rank = owned_ref.shape[0]
    start = dot(gram_ref[...], time_ref[...])
    basis = dot(start, orth_factor(dot(start, start, ((0,), (0,)))))
    time_out_ref[...] = basis * math.sqrt(groups_n)
    wide = dot(spread(groups_n, rank), basis)
    mixer = jnp.where(same_slot(groups_n, rank), dot(wide, wide, ((1,), (1,))), 0.0)
    out_ref[...] = dot(mixer, owned_ref[...])


def mix(gram, time_factor, owned):
    return pl.pallas_call(
        mix_kernel,
        out_shape=(jax.ShapeDtypeStruct(owned.shape, F32), jax.ShapeDtypeStruct(time_factor.shape, F32)),
        name="mix",
    )(gram, time_factor, owned)


def finish_kernel(scale, block_ref, mine_ref, other_ref, out_ref):
    factor = orth_factor(mine_ref[...] + other_ref[...]) * scale
    out_ref[...] = dot(block_ref[...], factor)


def finish(block, mine, other, scale):
    return pl.pallas_call(
        functools.partial(finish_kernel, scale), out_shape=jax.ShapeDtypeStruct(block.shape, F32), name="finish"
    )(block, mine, other)


def row_gram_kernel(block_ref, out_ref):
    block = block_ref[...]
    out_ref[...] = dot(block, block, ((0,), (0,)))


def row_gram(block):
    rank = block.shape[1]
    return pl.pallas_call(row_gram_kernel, out_shape=jax.ShapeDtypeStruct((rank, rank), F32), name="row_gram")(block)


def sum_of_small(part, axes, devices):
    if devices * part.size > 1 << 20:
        return lax.psum(part, axes)
    copies = jnp.broadcast_to(part.reshape(1, -1), (devices, part.size))
    received = lax.all_to_all(copies, axes, split_axis=0, concat_axis=0, tiled=True)
    return jnp.sum(received, axis=0).reshape(part.shape)


def make_on_device(groups_n, reps):
    half_n = groups_n // 2
    halves = [[h * half_n + i for i in range(half_n)] for h in range(2)]
    across = [(i, (i + half_n) % groups_n) for i in range(groups_n)]
    swap = [(0, 1), (1, 0)]

    def all_to_all(value, parts, groups=None):
        shape = value.shape
        value = value.reshape((parts, shape[0] // parts) + shape[1:])
        value = lax.all_to_all(value, "grp", split_axis=0, concat_axis=0, tiled=True, axis_index_groups=groups)
        return value.reshape(shape)

    def on_device(snapshots, row_factor, time_factor):
        rows, cols = snapshots.shape[1:]
        rank = row_factor.shape[1]
        width = cols // reps
        mine = lax.axis_index("rep").astype(jnp.int32).reshape(1)
        partner = 1 - mine
        image = snapshots[0]
        send = project(image, row_factor, partner, width)
        received = lax.ppermute(send, "rep", swap)
        summed = project(image, row_factor, mine, width) + received
        owned = all_to_all(summed, groups_n)
        gram_total = sum_of_small(small_gram(owned, groups_n), ("grp", "rep"), groups_n * reps)
        weights, new_time = mix(gram_total, time_factor, owned)
        weight = all_to_all(weights, groups_n)
        other_weight = lax.ppermute(weight, "rep", swap)
        product = multiply(image, other_weight, partner, multiply(image, weight, mine))
        parts = all_to_all(product, half_n, halves)
        chunk = jnp.sum(parts.reshape(half_n, rows // half_n, rank), axis=0)
        chunk = chunk + lax.ppermute(chunk, "grp", across)
        block = all_to_all(jnp.tile(chunk, (half_n, 1)), half_n, halves)
        gram = row_gram(block)
        new_rows = finish(block, gram, lax.ppermute(gram, "rep", swap), math.sqrt(rows * reps))
        return (new_rows, new_time)

    return on_device


def solution(mesh):
    return jax.shard_map(
        make_on_device(mesh.shape["grp"], mesh.shape["rep"]),
        mesh=mesh,
        in_specs=(P("grp", "rep", None), P("rep", None), P()),
        out_specs=(P("rep", None), P()),
        check_vma=False,
    )
```

time: 99.3 us -> 113 us (1.14)
  Pallas kernels: 0 us -> 32.2 us
  matrix products: 20.1 us -> 0 us
  blocking collectives: 63.6 us -> 56.4 us
  waiting for transfers between devices: 8.73 us -> 12.7 us
  local copies, waits for them, and re-layouts: 1.58 us -> 5.48 us
  starting transfers between devices: 1.77 us -> 3.64 us
  between operations: 2.33 us -> 0.69 us
    pallas_call x0 -> x8, Pallas kernels: none -> 32.2 us  [the longest x2 8.42 us: multiply(): pl.pallas_call(product_kernel, grid_spec=pltpu.PrefetchScalarGridSpec(num...]
    dot_general x46 -> x0, matrix products: 20.1 us -> none  [the longest x44 12.2 us: highdot(): jnp.dot(left, right, precision=HIGHEST, preferred_element_type=jnp.float32)]
    all_to_all x5 -> x4, blocking collectives: 63.6 us -> 56.4 us  [all_to_all(): lax.all_to_all(value, 'grp', split_axis=0, concat_axis=0, tiled=True, axi...]
    all_to_all x0 -> x1, waiting for transfers between devices: none -> 6.58 us  [sum_of_small(): lax.all_to_all(copies, axes, split_axis=0, concat_axis=0, tiled=True)]
    ppermute x3, waiting for transfers between devices: 3.94 us -> 0.8 us  [the longest x1 0.8 us: on_device(): lax.ppermute(gram, 'rep', swap)]
    all_to_all x0 -> x1, starting transfers between devices: none -> 2.57 us  [sum_of_small(): lax.all_to_all(copies, axes, split_axis=0, concat_axis=0, tiled=True)]
    unnamed x4 -> x12, local copies, waits for them, and re-layouts: 1.03 us -> 3.36 us
    broadcast_in_dim x2, local copies, waits for them, and re-layouts: 0.13 us -> 1.41 us  [sum_of_small(): copies = jnp.broadcast_to(part.reshape(1, -1), (devices, part.size))]
  transfers between devices with their start and end apart: 4 -> 5, of which waited for: 4 -> 3; matrix products, arithmetic and copies ran while one was open for 0% -> 1% of each run, Pallas kernels for 0% -> 7%
where the time goes in v1:
time: 113 us; the launch traced here: 112 us
  blocking collectives  56.4 us (50%)
  Pallas kernels  32.2 us (28%)
  waiting for transfers between devices  12.7 us (11%)
  local copies, waits for them, and re-layouts  5.48 us (5%)
  starting transfers between devices  3.64 us (3%)
    all_to_all x4, blocking collectives, all_to_all(): lax.all_to_all(value, 'grp', split_axis=0, concat_axis=0, tiled=True, axi...  56.4 us
    pallas_call x2, Pallas kernels, multiply(): pl.pallas_call(product_kernel, grid_spec=pltpu.PrefetchScalarGridSpec(num...  8.42 us
    pallas_call x2, Pallas kernels, project(): pl.pallas_call(project_kernel, grid_spec=pltpu.PrefetchScalarGridSpec(num...  7.71 us
    all_to_all x1, waiting for transfers between devices, sum_of_small(): lax.all_to_all(copies, axes, split_axis=0, concat_axis=0, tiled=True)  6.58 us
    pallas_call x1, Pallas kernels, finish(): pl.pallas_call(functools.partial(finish_kernel, scale), out_shape=jax.Sha...  6.04 us
    ppermute x1, waiting for transfers between devices, on_device(): chunk = chunk + lax.ppermute(chunk, 'grp', across)  5.35 us
    pallas_call x1, Pallas kernels, mix(): pl.pallas_call(mix_kernel, out_shape=(jax.ShapeDtypeStruct(owned.shape, F...  5.35 us
    unnamed x12, local copies, waits for them, and re-layouts  3.36 us
  transfers between devices with their start and end apart: 5, of which 3 were waited for; matrix products, arithmetic and copies ran while one was open for 1% of the time, Pallas kernels for 7%

profile of v1, /device:TPU:0, one launch (start us, length us, event | category | flops | bytes accessed | tf_op | source)
XLA Modules:
  0.0 112.3 jit_solution(10476456082247364785)
XLA Ops:
  0.6 3.9 %project.3 = f32[128,512]{1,0:T(8,128)} custom-call(s32[1]{0:T(128)S(6)} %sub.3.which_ref, f32[1024,1024]{1,0:T(8,128)} %bitcast.9, f32[1024,128]{1,0:T(8,128)} %factor_ref.3), custom_call_target="tpu_custom_call" | custom-call | flops 402653184 | bytes 2621440 | tf_op jit(solution)/shard_map/project/pallas_call | solution.py:70
  4.5 0.0 copy-start.4
  4.5 0.5 collective-permute-start
  5.0 3.8 %project.2 = f32[128,512]{1,0:T(8,128)} custom-call(s32[1]{0:T(128)} %bitcast.which_ref, f32[1024,1024]{1,0:T(8,128)} %bitcast.10, f32[1024,128]{1,0:T(8,128)} %factor_ref.3), custom_call_target="tpu_custom_call" | custom-call | flops 402653184 | bytes 2621440 | tf_op jit(solution)/shard_map/project/pallas_call | solution.py:70
  8.8 0.0 collective-permute-done
  8.8 1.0 add_bitcast_fusion
  9.8 18.3 %all_to_all.26 = f32[16,8,512]{2,1,0:T(8,128)} all-to-all(f32[16,8,512]{2,1,0:T(8,128)S(1)} %add_bitcast_fusion), channel_id=1, replica_groups=mesh['grp'=16,'rep'=2] {'grp'}, dimensions={0} | all-to-all | bytes 524288 | tf_op jit(solution)/shard_map/all_to_all | solution.py:212
  28.1 2.4 %small_gram.1 = f32[16,16]{1,0:T(8,128)} custom-call(f32[128,512]{1,0:T(8,128)} %bitcast.15), custom_call_target="tpu_custom_call" | custom-call | tf_op jit(solution)/shard_map/small_gram/pallas_call | solution.py:150
  30.5 0.8 broadcast_in_dim.7
  31.3 0.6 broadcast_in_dim.8
  31.9 2.6 %all-to-all-start.1 = ((f32[32,1,256]{2,1,0:T(1,128)}), f32[32,1,256]{2,1,0:T(1,128)S(1)}, u32[]{:S(2)}, u32[]{:S(2)}) async-start(f32[32,1,256]{2,1,0:T(1,128)} %broadcast_in_dim.8), calls=%async_computation.1 | async-start | bytes 65536 | tf_op jit(solution)/shard_map/all_to_all | solution.py:199
  34.5 0.0 copy-done.4
  34.5 0.7 copy.10.time_ref
  35.2 6.6 %all-to-all-done.1 = f32[32,1,256]{2,1,0:T(1,128)S(1)} async-done(((f32[32,1,256]{2,1,0:T(1,128)}), f32[32,1,256]{2,1,0:T(1,128)S(1)}, u32[]{:S(2)}, u32[]{:S(2)}) %all-to-all-start.1) | async-done | bytes 32800 | tf_op jit(solution)/shard_map/all_to_all | solution.py:199
  41.8 0.1 reduce_sum.18
  41.8 0.7 reshape.43.gram_ref
  42.5 5.4 %mix.1 = (f32[128,512]{1,0:T(8,128)}, f32[16,8]{1,0:T(8,128)}) custom-call(f32[16,16]{1,0:T(8,128)} %reshape.43.gram_ref, f32[16,8]{1,0:T(8,128)} %copy.10.time_ref, f32[128,512]{1,0:T(8,128)} %bitcast.16), custom_call_target="tpu_custom_call" | custom-call | tf_op jit(solution)/shard_map/mix/pallas_call | solution.py:167
  47.9 13.9 %all_to_all.27 = f32[16,8,512]{2,1,0:T(8,128)S(1)} all-to-all(f32[16,8,512]{2,1,0:T(8,128)} %bitcast.20), channel_id=1, replica_groups=mesh['grp'=16,'rep'=2] {'grp'}, dimensions={0} | all-to-all | bytes 524288 | tf_op jit(solution)/shard_map/all_to_all | solution.py:212
  61.8 0.0 copy-start
  61.8 0.0 collective-permute-start.1
  61.8 0.7 copy-done
  62.5 4.2 %multiply.2.refs_0_ = f32[1024,128]{1,0:T(8,128)} custom-call(s32[1]{0:T(128)} %bitcast.which_ref, f32[1024,1024]{1,0:T(8,128)} %bitcast.11, f32[128,512]{1,0:T(8,128)} %bitcast.19), custom_call_target="tpu_custom_call" | custom-call | flops 402653184 | bytes 2621440 | tf_op jit(solution)/shard_map/multiply/pallas_call | solution.py:108
  66.6 0.0 copy-start.3
  66.7 0.0 collective-permute-done.1.weight_ref
  66.7 0.0 copy-start.1
  66.7 0.7 copy-done.1
  67.4 4.2 %multiply.3 = f32[1024,128]{1,0:T(8,128)} custom-call(s32[1]{0:T(128)S(6)} %sub.3.which_ref, f32[1024,1024]{1,0:T(8,128)} %bitcast.12, f32[128,512]{1,0:T(8,128)} %copy-done.1, f32[1024,128]{1,0:T(8,128)} %multiply.2.refs_0_), custom_call_target="tpu_custom_call" | custom-call | flops 402653184 | bytes 2621440 | tf_op jit(solution)/shard_map/multiply/pallas_call | solution.py:108
  71.6 13.1 %all_to_all.28 = f32[8,128,128]{2,1,0:T(8,128)S(1)} all-to-all(f32[8,128,128]{2,1,0:T(8,128)} %bitcast.17), channel_id=1, replica_groups={{0,2,4,6,8,10,12,14},{16,18,20,22,24,26,28,30},{1,3,5,7,9,11,13,15},{17..., dimensions={0} | all-to-all | bytes 1048576 | tf_op jit(solution)/shard_map/all_to_all | solution.py:212
  84.7 0.6 collective-permute-start.2
  85.3 5.4 %collective-permute-done.2 = f32[128,128]{1,0:T(8,128)S(1)} collective-permute-done((f32[128,128]{1,0:T(8,128)S(1)}, f32[128,128]{1,0:T(8,128)S(1)}, u32[]{:S(2)}, u32[]{:S(2)}) %collective-permute-start.2) | collective-permute-done | bytes 65568 | tf_op jit(solution)/shard_map/ppermute | solution.py:233
  90.7 11.1 %all_to_all.29 = f32[8,128,128]{2,1,0:T(8,128)} all-to-all(f32[8,128,128]{2,1,0:T(8,128)S(1)} %reshape_tile.3), channel_id=1, replica_groups={{0,2,4,6,8,10,12,14},{16,18,20,22,24,26,28,30},{1,3,5,7,9,11,13,15},{17..., dimensions={0} | all-to-all | bytes 1048576 | tf_op jit(solution)/shard_map/all_to_all | solution.py:212
  101.8 2.3 %row_gram.1.mine_ref = f32[128,128]{1,0:T(8,128)} custom-call(f32[1024,128]{1,0:T(8,128)} %bitcast.13), custom_call_target="tpu_custom_call" | custom-call | tf_op jit(solution)/shard_map/row_gram/pallas_call | solution.py:192
  104.1 0.0 collective-permute-start.3
  104.1 0.0 copy-done.3
  104.1 0.7 copy.11
  104.8 0.8 collective-permute-done.3.other_ref
  105.6 0.0 copy-start.2
  105.6 0.6 copy-done.2
  106.2 6.0 %finish.1 = f32[1024,128]{1,0:T(8,128)} custom-call(f32[1024,128]{1,0:T(8,128)} %bitcast.14, f32[128,128]{1,0:T(8,128)} %row_gram.1.mine_ref, f32[128,128]{1,0:T(8,128)} %copy-done.2), custom_call_target="tpu_custom_call" | custom-call | tf_op jit(solution)/shard_map/finish/pallas_call | solution.py:180
  (3 shorter events, 0.1 us)
Async XLA Ops:
  4.5 30.0 %copy-start.4 = (f32[16,8]{0,1:T(8,128)S(1)}, f32[16,8]{0,1:T(8,128)}, u32[]{:S(2)}) copy-start(f32[16,8]{0,1:T(8,128)} %param.5) | copy-start | bytes 1540
  4.5 4.3 %collective-permute-start = (f32[128,512]{1,0:T(8,128)}, f32[128,512]{1,0:T(8,128)S(1)}, u32[]{:S(2)}, u32[]{:S(2)}) collective-permute-start(f32[128,512]{1,0:T(8,128)} %project.3), channel_id=1, source_target_pairs={{0,1},{1,0},{2,3},{3,2},{4,5},{5,4},{6,7},{7,6},{8,9},{9,8},{10,11... | collective-permute-start | bytes 786440 | tf_op jit(solution)/shard_map/ppermute | solution.py:223
  31.9 9.8 %all-to-all-start.1 = ((f32[32,1,256]{2,1,0:T(1,128)}), f32[32,1,256]{2,1,0:T(1,128)S(1)}, u32[]{:S(2)}, u32[]{:S(2)}) async-start(f32[32,1,256]{2,1,0:T(1,128)} %broadcast_in_dim.8), calls=%async_computation.1 | async-start | bytes 65536 | tf_op jit(solution)/shard_map/all_to_all | solution.py:199
  61.8 0.7 copy-start
  61.8 4.9 %collective-permute-start.1 = (f32[128,512]{1,0:T(8,128)S(1)}, f32[128,512]{1,0:T(8,128)S(1)}, u32[]{:S(2)}, u32[]{:S(2)}) collective-permute-start(f32[128,512]{1,0:T(8,128)S(1)} %bitcast.18), channel_id=1, source_target_pairs={{0,1},{1,0},{2,3},{3,2},{4,5},{5,4},{6,7},{7,6},{8,9},{9,8},{10,11... | collective-permute-start | bytes 786440 | tf_op jit(solution)/shard_map/ppermute | solution.py:229
  66.6 37.5 %copy-start.3 = (f32[16,8]{1,0:T(8,128)S(1)}, f32[16,8]{1,0:T(8,128)}, u32[]{:S(2)}) copy-start(f32[16,8]{1,0:T(8,128)} %get-tuple-element.11) | copy-start | bytes 1540
  66.7 0.7 copy-start.1
  84.7 5.9 %collective-permute-start.2 = (f32[128,128]{1,0:T(8,128)S(1)}, f32[128,128]{1,0:T(8,128)S(1)}, u32[]{:S(2)}, u32[]{:S(2)}) collective-permute-start(f32[128,128]{1,0:T(8,128)S(1)} %reduce_sum.19), channel_id=1, source_target_pairs={{0,16},{2,18},{4,20},{6,22},{8,24},{10,26},{12,28},{14,30},{16,0},... | collective-permute-start | bytes 196616 | tf_op jit(solution)/shard_map/ppermute | solution.py:233
  104.1 1.5 %collective-permute-start.3 = (f32[128,128]{1,0:T(8,128)}, f32[128,128]{1,0:T(8,128)S(1)}, u32[]{:S(2)}, u32[]{:S(2)}) collective-permute-start(f32[128,128]{1,0:T(8,128)} %row_gram.1.mine_ref), channel_id=1, source_target_pairs={{0,1},{1,0},{2,3},{3,2},{4,5},{5,4},{6,7},{7,6},{8,9},{9,8},{10,11... | collective-permute-start | bytes 196616 | tf_op jit(solution)/shard_map/ppermute | solution.py:236
  105.6 0.6 copy-start.2

commit v2 on v1

v2 whole, which is shorter than its diff:
```python
import functools
import math

import jax
import jax.numpy as jnp
from jax import lax
from jax.experimental import pallas as pl
from jax.experimental.pallas import tpu as pltpu
from jax.sharding import PartitionSpec as P

STEPS = 8
SMALL = pltpu.CompilerParams(vmem_limit_bytes=16 << 20)
F32 = jnp.float32
BF16 = jnp.bfloat16
TINY = 1e-06


def dot(left, right, contract=((1,), (0,))):
    return lax.dot_general(
        left, right, (contract, ((), ())), precision=lax.Precision.HIGHEST, preferred_element_type=F32
    )


def fastdot(left, right, contract):
    return lax.dot_general(left, right, (contract, ((), ())), preferred_element_type=F32)


def split(value):
    high = value.astype(BF16)
    return high, (value - high.astype(F32)).astype(BF16)


def eye(size):
    return (lax.broadcasted_iota(jnp.int32, (size, size), 0) == lax.broadcasted_iota(jnp.int32, (size, size), 1)).astype(F32)


def orth_factor(gram):
    unit = eye(gram.shape[0])
    total = jnp.sum(gram * unit) + TINY
    squared = gram * (1.0 / total)
    factor = unit * lax.rsqrt(total)
    for step_index in range(STEPS):
        turn = 1.5 * unit - 0.5 * squared
        factor = dot(factor, turn)
        if step_index < STEPS - 1:
            squared = dot(dot(squared, turn), turn)
    return factor


def project_block(image, factor):
    image_high, image_low = split(image)
    factor_high, factor_low = split(factor)
    rank = factor_high.shape[1]
    both = jnp.concatenate([factor_high, factor_low], axis=1)
    wide = fastdot(both, image_high, ((0,), (0,)))
    return wide[:rank] + wide[rank:] + fastdot(factor_high, image_low, ((0,), (0,)))


def first_kernel(which_ref, image_ref, factor_ref, out_ref, held_ref, factor_held_ref, image_sems, factor_sem):
    parts, blocks = image_sems.shape
    rows, width = held_ref.shape[1:]
    block = rows // blocks
    factor_copy = pltpu.make_async_copy(factor_ref, factor_held_ref, factor_sem)
    factor_copy.start()
    copies = []
    for part in range(parts):
        at = pl.multiple_of(which_ref[part] * width, width)
        for i in range(blocks):
            copy = pltpu.make_async_copy(
                image_ref.at[pl.ds(i * block, block), pl.ds(at, width)],
                held_ref.at[part, pl.ds(i * block, block)],
                image_sems.at[part, i],
            )
            copy.start()
            copies.append(copy)
    factor_copy.wait()
    for i in range(blocks):
        copies[i].wait()
        take = pl.ds(i * block, block)
        value = project_block(held_ref[0, take], factor_held_ref[take])
        if i == 0:
            out_ref[...] = value
        else:
            out_ref[...] += value
    for copy in copies[blocks:]:
        copy.wait()


def project_first(image, row_factor, order, width, blocks=4):
    rows = image.shape[0]
    rank = row_factor.shape[1]
    parts = image.shape[1] // width
    return pl.pallas_call(
        first_kernel,
        in_specs=[
            pl.BlockSpec(memory_space=pltpu.SMEM),
            pl.BlockSpec(memory_space=pl.ANY),
            pl.BlockSpec(memory_space=pl.ANY),
        ],
        out_shape=(
            jax.ShapeDtypeStruct((rank, width), F32),
            jax.ShapeDtypeStruct((parts, rows, width), F32),
            jax.ShapeDtypeStruct((rows, rank), F32),
        ),
        scratch_shapes=[pltpu.SemaphoreType.DMA((parts, blocks)), pltpu.SemaphoreType.DMA],
        compiler_params=SMALL,
        name="project_first",
    )(
        order,
        pltpu.with_memory_space_constraint(image, pltpu.HBM),
        pltpu.with_memory_space_constraint(row_factor, pltpu.HBM),
    )


def second_kernel(blocks, held_ref, factor_ref, out_ref):
    block = factor_ref.shape[0] // blocks
    total = None
    for i in range(blocks):
        take = pl.ds(i * block, block)
        value = project_block(held_ref[1, take], factor_ref[take])
        total = value if total is None else total + value
    out_ref[...] = total


def project_second(held, row_factor, blocks=4):
    rows, width = held.shape[1:]
    rank = row_factor.shape[1]
    return pl.pallas_call(
        functools.partial(second_kernel, blocks),
        out_shape=jax.ShapeDtypeStruct((rank, width), F32),
        cost_estimate=pl.CostEstimate(
            flops=6 * rows * width * rank, bytes_accessed=4 * rows * (width + rank), transcendentals=0
        ),
        compiler_params=SMALL,
        name="project_second",
    )(held, row_factor)


def product_kernel(part, blocks, held_ref, weight_ref, *refs):
    out_ref = refs[-1]
    weight_high, weight_low = split(weight_ref[...])
    rank = weight_high.shape[0]
    both = jnp.concatenate([weight_high, weight_low], axis=0)
    block = out_ref.shape[0] // blocks
    for i in range(blocks):
        take = pl.ds(i * block, block)
        image_high, image_low = split(held_ref[part, take])
        wide = fastdot(image_high, both, ((1,), (1,)))
        value = wide[:, :rank] + wide[:, rank:] + fastdot(image_low, weight_high, ((1,), (1,)))
        if len(refs) > 1:
            value = value + refs[0][take]
        out_ref[take] = value


def multiply(held, weight, part, start=None, blocks=4):
    rows, width = held.shape[1:]
    rank = weight.shape[0]
    more = () if start is None else (start,)
    return pl.pallas_call(
        functools.partial(product_kernel, part, blocks),
        out_shape=jax.ShapeDtypeStruct((rows, rank), F32),
        cost_estimate=pl.CostEstimate(
            flops=6 * rows * width * rank, bytes_accessed=4 * rows * (width + rank), transcendentals=0
        ),
        compiler_params=SMALL,
        name="multiply",
    )(held, weight, *more)


def spread(groups_n, rank):
    rows = lax.broadcasted_iota(jnp.int32, (rank, groups_n), 0) // (rank // groups_n)
    return (rows == lax.broadcasted_iota(jnp.int32, (rank, groups_n), 1)).astype(F32)


def same_slot(groups_n, rank):
    per = rank // groups_n
    left = lax.broadcasted_iota(jnp.int32, (rank, rank), 0) % per
    right = lax.broadcasted_iota(jnp.int32, (rank, rank), 1) % per
    return left == right


def cell_rows(groups_n, cells):
    rows = lax.broadcasted_iota(jnp.int32, (groups_n, cells), 0)
    return (rows == lax.broadcasted_iota(jnp.int32, (groups_n, cells), 1) // groups_n).astype(F32)


def cell_columns(groups_n, cells):
    columns = lax.broadcasted_iota(jnp.int32, (groups_n, cells), 0)
    return (columns == lax.broadcasted_iota(jnp.int32, (groups_n, cells), 1) % groups_n).astype(F32)


def gram_of(owned, groups_n):
    rank = owned.shape[0]
    full = jnp.where(same_slot(groups_n, rank), dot(owned, owned, ((1,), (1,))), 0.0)
    fold = spread(groups_n, rank)
    return dot(dot(fold, full, ((0,), (0,))), fold)


def gram_kernel(groups_n, owned_ref, out_ref):
    gram = gram_of(owned_ref[...], groups_n)
    if len(out_ref.shape) == 2:
        out_ref[...] = gram
    else:
        cells = out_ref.shape[2]
        flat = jnp.sum(cell_rows(groups_n, cells) * dot(gram, cell_columns(groups_n, cells)), axis=0, keepdims=True)
        out_ref[...] = jnp.broadcast_to(flat[None], out_ref.shape)


def small_gram(owned, groups_n, shape):
    return pl.pallas_call(
        functools.partial(gram_kernel, groups_n),
        out_shape=jax.ShapeDtypeStruct(shape, F32),
        compiler_params=SMALL,
        name="small_gram",
    )(owned)


def mix_kernel(groups_n, gram_ref, time_ref, owned_ref, out_ref, time_out_ref):
    rank = owned_ref.shape[0]
    if len(gram_ref.shape) == 2:
        gram = gram_ref[...]
    else:
        cells = gram_ref.shape[2]
        flat = jnp.sum(gram_ref[...], axis=0)
        gram = dot(cell_rows(groups_n, cells) * flat, cell_columns(groups_n, cells), ((1,), (1,)))
    start = dot(gram, time_ref[...], ((1,), (1,)))
    basis = dot(start, orth_factor(dot(start, start, ((0,), (0,)))))
    time_out_ref[...] = basis * math.sqrt(groups_n)
    wide = dot(spread(groups_n, rank), basis)
    mixer = jnp.where(same_slot(groups_n, rank), dot(wide, wide, ((1,), (1,))), 0.0)
    out_ref[...] = dot(mixer, owned_ref[...])


def mix(gram, time_factor, owned, groups_n):
    return pl.pallas_call(
        functools.partial(mix_kernel, groups_n),
        out_shape=(jax.ShapeDtypeStruct(owned.shape, F32), jax.ShapeDtypeStruct(time_factor.shape, F32)),
        compiler_params=SMALL,
        name="mix",
    )(gram, time_factor.T, owned)


def finish_kernel(scale, block_ref, mine_ref, other_ref, out_ref):
    factor = orth_factor(mine_ref[...] + other_ref[...]) * scale
    out_ref[...] = dot(block_ref[...], factor)


def finish(block, mine, other, scale):
    return pl.pallas_call(
        functools.partial(finish_kernel, scale), out_shape=jax.ShapeDtypeStruct(block.shape, F32), compiler_params=SMALL, name="finish"
    )(block, mine, other)


def row_gram_kernel(block_ref, out_ref):
    block = block_ref[...]
    out_ref[...] = dot(block, block, ((0,), (0,)))


def row_gram(block):
    rank = block.shape[1]
    return pl.pallas_call(row_gram_kernel, out_shape=jax.ShapeDtypeStruct((rank, rank), F32), compiler_params=SMALL, name="row_gram")(block)


def make_on_device(groups_n, reps):
    half_n = groups_n // 2
    halves = [[h * half_n + i for i in range(half_n)] for h in range(2)]
    across = [(i, (i + half_n) % groups_n) for i in range(groups_n)]
    swap = [(0, 1), (1, 0)]

    def all_to_all(value, parts, groups=None):
        shape = value.shape
        value = value.reshape((parts, shape[0] // parts) + shape[1:])
        value = lax.all_to_all(value, "grp", split_axis=0, concat_axis=0, tiled=True, axis_index_groups=groups)
        return value.reshape(shape)

    def on_device(snapshots, row_factor, time_factor):
        rows, cols = snapshots.shape[1:]
        rank = row_factor.shape[1]
        width = cols // reps
        mine = lax.axis_index("rep").astype(jnp.int32)
        order = jnp.stack([1 - mine, mine])
        send, held, factor = project_first(snapshots[0], row_factor, order, width)
        received = lax.ppermute(send, "rep", swap)
        summed = project_second(held, factor) + received
        owned = all_to_all(summed, groups_n)
        devices = groups_n * reps
        if devices * groups_n * groups_n <= 1 << 20:
            grams = lax.all_to_all(
                small_gram(owned, groups_n, (devices, 1, groups_n * groups_n)),
                ("grp", "rep"),
                split_axis=0,
                concat_axis=0,
                tiled=True,
            )
        else:
            grams = lax.psum(small_gram(owned, groups_n, (groups_n, groups_n)), ("grp", "rep"))
        weights, new_time = mix(grams, time_factor, owned, groups_n)
        weight = all_to_all(weights, groups_n)
        other_weight = lax.ppermute(weight, "rep", swap)
        product = multiply(held, other_weight, 0, multiply(held, weight, 1))
        parts = all_to_all(product, half_n, halves)
        chunk = jnp.sum(parts.reshape(half_n, rows // half_n, rank), axis=0)
        chunk = chunk + lax.ppermute(chunk, "grp", across)
        block = all_to_all(jnp.tile(chunk, (half_n, 1)), half_n, halves)
        gram = row_gram(block)
        new_rows = finish(block, gram, lax.ppermute(gram, "rep", swap), math.sqrt(rows * reps))
        return (new_rows, new_time)

    return on_device


def solution(mesh):
    return jax.shard_map(
        make_on_device(mesh.shape["grp"], mesh.shape["rep"]),
        mesh=mesh,
        in_specs=(P("grp", "rep", None), P("rep", None), P()),
        out_specs=(P("rep", None), P()),
        check_vma=False,
    )
```

time: 113 us -> 90.2 us (0.80)
  Pallas kernels: 32.2 us -> 16.3 us
  blocking collectives: 56.4 us -> 63.7 us
  waiting for transfers between devices: 12.7 us -> 6.68 us
  local copies, waits for them, and re-layouts: 5.48 us -> 0.7 us
  starting transfers between devices: 3.64 us -> 1.76 us
    pallas_call x6, Pallas kernels: 23.9 us -> 10.7 us  [the longest x1 3.86 us: mix(): pl.pallas_call(functools.partial(mix_kernel, groups_n), out_shape=(jax.Sh...]
    all_to_all x0 -> x1, blocking collectives: none -> 9.59 us  [on_device(): lax.all_to_all(small_gram(owned, groups_n, (devices, 1, groups_n * groups...]
    all_to_all x1 -> x0, waiting for transfers between devices: 6.58 us -> none  [sum_of_small(): lax.all_to_all(copies, axes, split_axis=0, concat_axis=0, tiled=True)]
    unnamed x12 -> x3, local copies, waits for them, and re-layouts: 3.36 us -> 0.67 us
    all_to_all x1 -> x0, starting transfers between devices: 2.57 us -> none  [sum_of_small(): lax.all_to_all(copies, axes, split_axis=0, concat_axis=0, tiled=True)]
    all_to_all x4, blocking collectives: 56.4 us -> 54.1 us  [all_to_all(): lax.all_to_all(value, 'grp', split_axis=0, concat_axis=0, tiled=True, axi...]
    pallas_call x1, Pallas kernels: 2.31 us -> 0.64 us  [row_gram(): pl.pallas_call(row_gram_kernel, out_shape=jax.ShapeDtypeStruct((rank, ran...]
    broadcast_in_dim x2 -> x0, local copies, waits for them, and re-layouts: 1.41 us -> none  [sum_of_small(): copies = jnp.broadcast_to(part.reshape(1, -1), (devices, part.size))]
  transfers between devices with their start and end apart: 5 -> 4, of which waited for: 3 -> 4; matrix products, arithmetic and copies ran while one was open for 1% -> 1% of each run, Pallas kernels for 7% -> 2%
where the time goes in v2:
time: 90.2 us; the launch traced here: 89.9 us
  blocking collectives  63.7 us (71%)
  Pallas kernels  16.3 us (18%)
  waiting for transfers between devices  6.68 us (7%)
  starting transfers between devices  1.76 us (2%)
    all_to_all x4, blocking collectives, all_to_all(): lax.all_to_all(value, 'grp', split_axis=0, concat_axis=0, tiled=True, axi...  54.1 us
    all_to_all x1, blocking collectives, on_device(): lax.all_to_all(small_gram(owned, groups_n, (devices, 1, groups_n * groups...  9.59 us
    pallas_call x1, Pallas kernels, finish(): pl.pallas_call(functools.partial(finish_kernel, scale), out_shape=jax.Sha...  4.96 us
    ppermute x1, waiting for transfers between devices, on_device(): chunk = chunk + lax.ppermute(chunk, 'grp', across)  4.81 us
    pallas_call x1, Pallas kernels, mix(): pl.pallas_call(functools.partial(mix_kernel, groups_n), out_shape=(jax.Sh...  3.86 us
    pallas_call x1, Pallas kernels, project_first(): pl.pallas_call(first_kernel, in_specs=[pl.BlockSpec(memory_space=pltpu.SM...  3.63 us
  transfers between devices with their start and end apart: 4, of which 4 were waited for; matrix products, arithmetic and copies ran while one was open for 1% of the time, Pallas kernels for 2%

profile of v2, /device:TPU:0, one launch (start us, length us, event | category | flops | bytes accessed | tf_op | source)
XLA Modules:
  0.0 89.9 jit_solution(15782693976760178394)
XLA Ops:
  0.6 0.1 pad_add_fusion.which_ref
  0.7 3.6 %project_first.1 = (f32[128,512]{1,0:T(8,128)S(1)}, f32[2,1024,512]{2,1,0:T(8,128)S(1)}, f32[1024,128]{1,0:T(8,128)S(1)}) custom-call(s32[2]{0:T(128)S(1)} %pad_add_fusion.which_ref, f32[1024,1024]{1,0:T(8,128)} %bitcast.20, f32[1024,128]{1,0:T(8,128)} %factor_ref.1), custom_call_target="tpu_custom_call" | custom-call | tf_op jit(solution)/shard_map/project_first/pallas_call | solution.py:93
  4.3 0.0 copy-start
  4.4 0.6 collective-permute-start
  4.9 0.7 project_second.1
  5.6 0.5 collective-permute-done
  6.1 18.2 %all_to_all.25 = f32[16,8,512]{2,1,0:T(8,128)S(1)} all-to-all(f32[16,8,512]{2,1,0:T(8,128)S(1)} %add_bitcast_fusion), channel_id=1, replica_groups=mesh['grp'=16,'rep'=2] {'grp'}, dimensions={0} | all-to-all | bytes 524288 | tf_op jit(solution)/shard_map/all_to_all | solution.py:273
  24.3 1.1 %small_gram.1 = f32[32,1,256]{2,1,0:T(1,128)S(1)} custom-call(f32[128,512]{1,0:T(8,128)S(1)} %bitcast.13), custom_call_target="tpu_custom_call" | custom-call | tf_op jit(solution)/shard_map/small_gram/pallas_call | solution.py:210
  25.4 9.6 %all_to_all.26.gram_ref = f32[32,1,256]{2,1,0:T(1,128)S(1)} all-to-all(f32[32,1,256]{2,1,0:T(1,128)S(1)} %small_gram.1), channel_id=1, replica_groups=mesh['grp'=16,'rep'=2] {'grp','rep'}, dimensions={0} | all-to-all | bytes 65536 | tf_op jit(solution)/shard_map/all_to_all | solution.py:288
  35.0 0.0 copy-done
  35.0 3.9 %mix.1 = (f32[128,512]{1,0:T(8,128)S(1)}, f32[16,8]{1,0:T(8,128)S(1)}) custom-call(f32[32,1,256]{2,1,0:T(1,128)S(1)} %all_to_all.26.gram_ref, f32[8,16]{1,0:T(8,128)S(1)} %bitcast.19, f32[128,512]{1,0:T(8,128)S(1)} %bitcast.14), custom_call_target="tpu_custom_call" | custom-call | tf_op jit(solution)/shard_map/mix/pallas_call | solution.py:235
  38.8 13.0 %all_to_all.27 = f32[16,8,512]{2,1,0:T(8,128)S(1)} all-to-all(f32[16,8,512]{2,1,0:T(8,128)S(1)} %bitcast.18), channel_id=1, replica_groups=mesh['grp'=16,'rep'=2] {'grp'}, dimensions={0} | all-to-all | bytes 524288 | tf_op jit(solution)/shard_map/all_to_all | solution.py:273
  51.9 0.0 collective-permute-start.1
  51.9 0.7 multiply.2.refs_0_
  52.6 0.8 collective-permute-done.1.weight_ref
  53.4 0.7 multiply.3
  54.1 12.4 %all_to_all.28 = f32[8,128,128]{2,1,0:T(8,128)S(1)} all-to-all(f32[8,128,128]{2,1,0:T(8,128)S(1)} %bitcast.15), channel_id=1, replica_groups={{0,2,4,6,8,10,12,14},{16,18,20,22,24,26,28,30},{1,3,5,7,9,11,13,15},{17..., dimensions={0} | all-to-all | bytes 1048576 | tf_op jit(solution)/shard_map/all_to_all | solution.py:273
  66.6 1.1 %collective-permute-start.2 = (f32[128,128]{1,0:T(8,128)S(1)}, f32[128,128]{1,0:T(8,128)S(1)}, u32[]{:S(2)}, u32[]{:S(2)}) collective-permute-start(f32[128,128]{1,0:T(8,128)S(1)} %reduce_sum.9), channel_id=1, source_target_pairs={{0,16},{2,18},{4,20},{6,22},{8,24},{10,26},{12,28},{14,30},{16,0},... | collective-permute-start | bytes 196616 | tf_op jit(solution)/shard_map/ppermute | solution.py:303
  67.7 4.8 %collective-permute-done.2 = f32[128,128]{1,0:T(8,128)S(1)} collective-permute-done((f32[128,128]{1,0:T(8,128)S(1)}, f32[128,128]{1,0:T(8,128)S(1)}, u32[]{:S(2)}, u32[]{:S(2)}) %collective-permute-start.2) | collective-permute-done | bytes 65568 | tf_op jit(solution)/shard_map/ppermute | solution.py:303
  72.6 10.4 %all_to_all.29 = f32[8,128,128]{2,1,0:T(8,128)S(1)} all-to-all(f32[8,128,128]{2,1,0:T(8,128)S(1)} %reshape_tile.3), channel_id=1, replica_groups={{0,2,4,6,8,10,12,14},{16,18,20,22,24,26,28,30},{1,3,5,7,9,11,13,15},{17..., dimensions={0} | all-to-all | bytes 1048576 | tf_op jit(solution)/shard_map/all_to_all | solution.py:273
  83.0 0.6 row_gram.1.mine_ref
  83.7 0.1 collective-permute-start.3
  83.7 0.7 copy.5
  84.4 0.6 collective-permute-done.3.other_ref
  85.0 5.0 %finish.1 = f32[1024,128]{1,0:T(8,128)} custom-call(f32[1024,128]{1,0:T(8,128)S(1)} %bitcast.12, f32[128,128]{1,0:T(8,128)S(1)} %row_gram.1.mine_ref, f32[128,128]{1,0:T(8,128)S(1)} %collective-permute-done.3.other_ref), custom_call_target="tpu_custom_call" | custom-call | tf_op jit(solution)/shard_map/finish/pallas_call | solution.py:249
  (4 shorter events, 0.1 us)
Async XLA Ops:
  4.3 30.6 %copy-start = (f32[16,8]{0,1:T(8,128)S(1)}, f32[16,8]{0,1:T(8,128)}, u32[]{:S(2)}) copy-start(f32[16,8]{0,1:T(8,128)} %param.5) | copy-start | bytes 1540
  4.4 1.7 %collective-permute-start = (f32[128,512]{1,0:T(8,128)S(1)}, f32[128,512]{1,0:T(8,128)S(1)}, u32[]{:S(2)}, u32[]{:S(2)}) collective-permute-start(f32[128,512]{1,0:T(8,128)S(1)} %get-tuple-element.9), channel_id=1, source_target_pairs={{0,1},{1,0},{2,3},{3,2},{4,5},{5,4},{6,7},{7,6},{8,9},{9,8},{10,11... | collective-permute-start | bytes 786440 | tf_op jit(solution)/shard_map/ppermute | solution.py:283
  51.9 1.5 %collective-permute-start.1 = (f32[128,512]{1,0:T(8,128)S(1)}, f32[128,512]{1,0:T(8,128)S(1)}, u32[]{:S(2)}, u32[]{:S(2)}) collective-permute-start(f32[128,512]{1,0:T(8,128)S(1)} %bitcast.16), channel_id=1, source_target_pairs={{0,1},{1,0},{2,3},{3,2},{4,5},{5,4},{6,7},{7,6},{8,9},{9,8},{10,11... | collective-permute-start | bytes 786440 | tf_op jit(solution)/shard_map/ppermute | solution.py:299
  66.6 5.9 %collective-permute-start.2 = (f32[128,128]{1,0:T(8,128)S(1)}, f32[128,128]{1,0:T(8,128)S(1)}, u32[]{:S(2)}, u32[]{:S(2)}) collective-permute-start(f32[128,128]{1,0:T(8,128)S(1)} %reduce_sum.9), channel_id=1, source_target_pairs={{0,16},{2,18},{4,20},{6,22},{8,24},{10,26},{12,28},{14,30},{16,0},... | collective-permute-start | bytes 196616 | tf_op jit(solution)/shard_map/ppermute | solution.py:303
  83.7 1.3 %collective-permute-start.3 = (f32[128,128]{1,0:T(8,128)S(1)}, f32[128,128]{1,0:T(8,128)S(1)}, u32[]{:S(2)}, u32[]{:S(2)}) collective-permute-start(f32[128,128]{1,0:T(8,128)S(1)} %row_gram.1.mine_ref), channel_id=1, source_target_pairs={{0,1},{1,0},{2,3},{3,2},{4,5},{5,4},{6,7},{7,6},{8,9},{9,8},{10,11... | collective-permute-start | bytes 196616 | tf_op jit(solution)/shard_map/ppermute | solution.py:306

commit v3 on v2

v3 whole, which is shorter than its diff:
```python
import functools
import math

import jax
import jax.numpy as jnp
from jax import lax
from jax.experimental import pallas as pl
from jax.experimental.pallas import tpu as pltpu
from jax.sharding import PartitionSpec as P

STEPS = 8
SMALL = pltpu.CompilerParams(vmem_limit_bytes=16 << 20)
F32 = jnp.float32
BF16 = jnp.bfloat16
TINY = 1e-06


def dot(left, right, contract=((1,), (0,))):
    return lax.dot_general(
        left, right, (contract, ((), ())), precision=lax.Precision.HIGHEST, preferred_element_type=F32
    )


def fastdot(left, right, contract):
    return lax.dot_general(left, right, (contract, ((), ())), preferred_element_type=F32)


def split(value):
    high = value.astype(BF16)
    return high, (value - high.astype(F32)).astype(BF16)


def eye(size):
    return (lax.broadcasted_iota(jnp.int32, (size, size), 0) == lax.broadcasted_iota(jnp.int32, (size, size), 1)).astype(F32)


def split3(value):
    high = value.astype(BF16)
    rest = value - high.astype(F32)
    middle = rest.astype(BF16)
    return high, middle, (rest - middle.astype(F32)).astype(BF16)


def left6(value):
    high, middle, low = split3(value)
    return jnp.concatenate([high, high, middle, high, middle, low], axis=1)


def right6(value):
    high, middle, low = split3(value)
    return jnp.concatenate([high, middle, high, low, middle, high], axis=0)


def times(right):
    size = right.shape[0]
    if size <= 16:
        rows = [right[k : k + 1, :] for k in range(size)]

        def apply(left):
            terms = [left[:, k : k + 1] * rows[k] for k in range(size)]
            while len(terms) > 1:
                terms = [sum(terms[i : i + 2]) for i in range(0, len(terms), 2)]
            return terms[0]

        return apply
    if size % 128 == 0:
        stacked = right6(right)
        return lambda left: fastdot(left6(left), stacked, ((1,), (0,)))
    return lambda left: dot(left, right)


def orth_factor(gram):
    unit = eye(gram.shape[0])
    total = jnp.sum(gram * unit) + TINY
    squared = gram * (1.0 / total)
    factor = unit * lax.rsqrt(total)
    for step_index in range(STEPS):
        turn = 1.5 * unit - 0.5 * squared
        by_turn = times(turn)
        factor = by_turn(factor) if step_index else factor[:1, :1] * turn
        if step_index < STEPS - 1:
            squared = by_turn(by_turn(squared))
    return factor


def halves_of(value):
    high, low = split(value)
    return jnp.concatenate([high, low], axis=1)


def project_block(image_high, image_low, factor_both):
    rank = factor_both.shape[1] // 2
    wide = fastdot(factor_both, image_high, ((0,), (0,)))
    return wide[:rank] + wide[rank:] + fastdot(factor_both[:, :rank], image_low, ((0,), (0,)))


def first_kernel(
    image_ref, factor_ref, out_ref, high_ref, low_ref, later_ref, both_ref, now_ref, fetched_ref, image_sems, factor_sem
):
    parts, blocks = image_sems.shape
    rows, width = now_ref.shape
    block = rows // blocks
    me = lax.axis_index("rep")
    factor_copy = pltpu.make_async_copy(factor_ref, fetched_ref, factor_sem)
    factor_copy.start()
    copies = []
    for part, held_ref in enumerate((now_ref, later_ref)):
        at = pl.multiple_of(lax.rem(me + 1 + part, parts) * width, width)
        for i in range(blocks):
            take = pl.ds(i * block, block)
            copy = pltpu.make_async_copy(image_ref.at[take, pl.ds(at, width)], held_ref.at[take], image_sems.at[part, i])
            copies.append(copy)
    for copy in copies[:blocks]:
        copy.start()
    factor_copy.wait()
    both_ref[...] = halves_of(fetched_ref[...])
    for i in range(blocks):
        copies[i].wait()
        copies[blocks + i].start()
        take = pl.ds(i * block, block)
        high, low = split(now_ref[take])
        high_ref[take] = high
        low_ref[take] = low
        value = project_block(high, low, both_ref[take])
        if i == 0:
            out_ref[...] = value
        else:
            out_ref[...] += value
    for copy in copies[blocks:]:
        copy.wait()


def project_first(image, row_factor, width, blocks=4):
    rows = image.shape[0]
    rank = row_factor.shape[1]
    parts = image.shape[1] // width
    return pl.pallas_call(
        first_kernel,
        in_specs=[pl.BlockSpec(memory_space=pl.ANY), pl.BlockSpec(memory_space=pl.ANY)],
        out_shape=(
            jax.ShapeDtypeStruct((rank, width), F32),
            jax.ShapeDtypeStruct((rows, width), BF16),
            jax.ShapeDtypeStruct((rows, width), BF16),
            jax.ShapeDtypeStruct((rows, width), F32),
            jax.ShapeDtypeStruct((rows, 2 * rank), BF16),
        ),
        scratch_shapes=[
            pltpu.VMEM((rows, width), F32),
            pltpu.VMEM((rows, rank), F32),
            pltpu.SemaphoreType.DMA((parts, blocks)),
            pltpu.SemaphoreType.DMA,
        ],
        compiler_params=SMALL,
        name="project_first",
    )(
        pltpu.with_memory_space_constraint(image, pltpu.HBM),
        pltpu.with_memory_space_constraint(row_factor, pltpu.HBM),
    )


def second_kernel(blocks, image_ref, both_ref, out_ref, high_ref, low_ref):
    block = image_ref.shape[0] // blocks
    total = None
    for i in range(blocks):
        take = pl.ds(i * block, block)
        high, low = split(image_ref[take])
        high_ref[take] = high
        low_ref[take] = low
        value = project_block(high, low, both_ref[take])
        total = value if total is None else total + value
    out_ref[...] = total


def project_second(image, both, blocks=4):
    rows, width = image.shape
    rank = both.shape[1] // 2
    return pl.pallas_call(
        functools.partial(second_kernel, blocks),
        out_shape=(
            jax.ShapeDtypeStruct((rank, width), F32),
            jax.ShapeDtypeStruct((rows, width), BF16),
            jax.ShapeDtypeStruct((rows, width), BF16),
        ),
        cost_estimate=pl.CostEstimate(
            flops=6 * rows * width * rank, bytes_accessed=4 * rows * (width + rank), transcendentals=0
        ),
        compiler_params=SMALL,
        name="project_second",
    )(image, both)


def product_kernel(blocks, high_ref, low_ref, weight_ref, *refs):
    out_ref = refs[-1]
    weight_high, weight_low = split(weight_ref[...])
    rank = weight_high.shape[0]
    both = jnp.concatenate([weight_high, weight_low], axis=0)
    block = out_ref.shape[0] // blocks
    for i in range(blocks):
        take = pl.ds(i * block, block)
        wide = fastdot(high_ref[take], both, ((1,), (1,)))
        value = wide[:, :rank] + wide[:, rank:] + fastdot(low_ref[take], weight_high, ((1,), (1,)))
        if len(refs) > 1:
            value = value + refs[0][take]
        out_ref[take] = value


def multiply(high, low, weight, start=None, blocks=4):
    rows, width = high.shape
    rank = weight.shape[0]
    more = () if start is None else (start,)
    return pl.pallas_call(
        functools.partial(product_kernel, blocks),
        out_shape=jax.ShapeDtypeStruct((rows, rank), F32),
        cost_estimate=pl.CostEstimate(
            flops=6 * rows * width * rank, bytes_accessed=4 * rows * (width + rank), transcendentals=0
        ),
        compiler_params=SMALL,
        name="multiply",
    )(high, low, weight, *more)


def cells(rows, count, row_of, cell_of):
    row = row_of(lax.broadcasted_iota(jnp.int32, (rows, count), 0))
    return (row == cell_of(lax.broadcasted_iota(jnp.int32, (rows, count), 1))).astype(F32)


def spread(groups_n, rank):
    per = rank // groups_n
    return cells(rank, groups_n, lambda row: row // per, lambda cell: cell)


def same_slot(groups_n, rank):
    per = rank // groups_n
    return cells(rank, rank, lambda row: row % per, lambda cell: cell % per) > 0.5


def gram_kernel(groups_n, owned_ref, out_ref):
    owned = owned_ref[...]
    rank = owned.shape[0]
    per = rank // groups_n
    full = jnp.where(same_slot(groups_n, rank), dot(owned, owned, ((1,), (1,))), 0.0)
    if len(out_ref.shape) == 2:
        fold = spread(groups_n, rank)
        out_ref[...] = dot(dot(fold, full, ((0,), (0,))), fold)
    else:
        count = out_ref.shape[2]
        columns = cells(rank, count, lambda row: row // per, lambda cell: cell % groups_n).astype(BF16)
        folded = fastdot(
            jnp.concatenate(split3(full), axis=1), jnp.concatenate([columns, columns, columns], axis=0), ((1,), (0,))
        )
        rows = cells(rank, count, lambda row: row // per, lambda cell: cell // groups_n)
        flat = jnp.sum(rows * folded, axis=0, keepdims=True)
        out_ref[...] = jnp.broadcast_to(flat[None], out_ref.shape)


def small_gram(owned, groups_n, shape):
    return pl.pallas_call(
        functools.partial(gram_kernel, groups_n),
        out_shape=jax.ShapeDtypeStruct(shape, F32),
        compiler_params=SMALL,
        name="small_gram",
    )(owned)


def mix_kernel(groups_n, gram_ref, time_ref, owned_ref, out_ref, time_out_ref):
    rank = owned_ref.shape[0]
    per = rank // groups_n
    if len(gram_ref.shape) == 2:
        fold = spread(groups_n, rank)
        start = dot(fold, dot(gram_ref[...], time_ref[...], ((1,), (1,))))
        turned = dot(dot(time_ref[...], gram_ref[...], ((1,), (1,))), fold, ((1,), (1,)))
    else:
        count = gram_ref.shape[2]
        flat = jnp.sum(gram_ref[...], axis=0)
        rows = cells(rank, count, lambda row: row // per, lambda cell: cell // groups_n) * flat
        columns = dot(time_ref[...], cells(groups_n, count, lambda row: row, lambda cell: cell % groups_n))
        start = dot(rows, columns, ((1,), (1,)))
        turned = dot(columns, rows, ((1,), (1,)))
    basis = dot(start, orth_factor(dot(turned, start) * (1.0 / per)))
    mixer = jnp.where(same_slot(groups_n, rank), dot(basis, basis, ((1,), (1,))), 0.0)
    mixer_high, mixer_low = split(mixer)
    owned_high, owned_low = split(owned_ref[...])
    out_ref[...] = fastdot(
        jnp.concatenate([mixer_high, mixer_low, mixer_high], axis=1),
        jnp.concatenate([owned_high, owned_high, owned_low], axis=0),
        ((1,), (0,)),
    )
    one_of_each = cells(groups_n, rank, lambda row: row * per, lambda cell: cell)
    time_out_ref[...] = dot(one_of_each, basis) * math.sqrt(groups_n)


def mix(gram, time_factor, owned, groups_n):
    return pl.pallas_call(
        functools.partial(mix_kernel, groups_n),
        out_shape=(jax.ShapeDtypeStruct(owned.shape, F32), jax.ShapeDtypeStruct(time_factor.shape, F32)),
        compiler_params=SMALL,
        name="mix",
    )(gram, time_factor.T, owned)


def finish_kernel(scale, blocks, block_ref, mine_ref, other_ref, out_ref, made_ref, sems):
    rows = block_ref.shape[0] // blocks
    high, low = split(block_ref[...])
    left = jnp.concatenate([high, low, high], axis=1)
    factor_high, factor_low = split(orth_factor(mine_ref[...] + other_ref[...]) * scale)
    right = jnp.concatenate([factor_high, factor_high, factor_low], axis=0)
    copies = []
    for i in range(blocks):
        take = pl.ds(i * rows, rows)
        made_ref[take] = fastdot(left[i * rows : (i + 1) * rows], right, ((1,), (0,)))
        copies.append(pltpu.make_async_copy(made_ref.at[take], out_ref.at[take], sems.at[i]))
        copies[-1].start()
    for copy in copies:
        copy.wait()


def finish(block, mine, other, scale, blocks=4):
    return pl.pallas_call(
        functools.partial(finish_kernel, scale, blocks),
        out_shape=jax.ShapeDtypeStruct(block.shape, F32),
        out_specs=pl.BlockSpec(memory_space=pl.ANY),
        scratch_shapes=[pltpu.VMEM(block.shape, F32), pltpu.SemaphoreType.DMA((blocks,))],
        compiler_params=SMALL,
        name="finish",
    )(block, mine, other)


def row_gram_kernel(block_ref, out_ref):
    block = block_ref[...]
    out_ref[...] = dot(block, block, ((0,), (0,)))


def row_gram(block):
    rank = block.shape[1]
    return pl.pallas_call(row_gram_kernel, out_shape=jax.ShapeDtypeStruct((rank, rank), F32), compiler_params=SMALL, name="row_gram")(block)


def make_on_device(groups_n, reps):
    half_n = groups_n // 2
    halves = [[h * half_n + i for i in range(half_n)] for h in range(2)]
    across = [(i, (i + half_n) % groups_n) for i in range(groups_n)]
    swap = [(0, 1), (1, 0)]

    def all_to_all(value, parts, groups=None):
        shape = value.shape
        value = value.reshape((parts, shape[0] // parts) + shape[1:])
        value = lax.all_to_all(value, "grp", split_axis=0, concat_axis=0, tiled=True, axis_index_groups=groups)
        return value.reshape(shape)

    def on_device(snapshots, row_factor, time_factor):
        rows, cols = snapshots.shape[1:]
        rank = row_factor.shape[1]
        width = cols // reps
        send, far_high, far_low, near, both = project_first(snapshots[0], row_factor, width)
        received = lax.ppermute(send, "rep", swap)
        summed, near_high, near_low = project_second(near, both)
        summed = summed + received
        owned = all_to_all(summed, groups_n)
        devices = groups_n * reps
        if devices * groups_n * groups_n <= 1 << 20:
            grams = lax.all_to_all(
                small_gram(owned, groups_n, (devices, 1, groups_n * groups_n)),
                ("grp", "rep"),
                split_axis=0,
                concat_axis=0,
                tiled=True,
            )
        else:
            grams = lax.psum(small_gram(owned, groups_n, (groups_n, groups_n)), ("grp", "rep"))
        weights, new_time = mix(grams, time_factor, owned, groups_n)
        weight = all_to_all(weights, groups_n)
        other_weight = lax.ppermute(weight, "rep", swap)
        product = multiply(far_high, far_low, other_weight, multiply(near_high, near_low, weight))
        parts = all_to_all(product, half_n, halves)
        chunk = jnp.sum(parts.reshape(half_n, rows // half_n, rank), axis=0)
        chunk = chunk + lax.ppermute(chunk, "grp", across)
        block = all_to_all(jnp.tile(chunk, (half_n, 1)), half_n, halves)
        gram = row_gram(block)
        new_rows = finish(block, gram, lax.ppermute(gram, "rep", swap), math.sqrt(rows * reps))
        return (new_rows, new_time)

    return on_device


def solution(mesh):
    return jax.shard_map(
        make_on_device(mesh.shape["grp"], mesh.shape["rep"]),
        mesh=mesh,
        in_specs=(P("grp", "rep", None), P("rep", None), P()),
        out_specs=(P("rep", None), P()),
        check_vma=False,
    )
```

time: 90.2 us -> 87.5 us (0.970)
  Pallas kernels: 16.3 us -> 13.6 us
    pallas_call x5, Pallas kernels: 10.7 us -> 9.42 us  [the longest x1 4.32 us: finish(): pl.pallas_call(functools.partial(finish_kernel, scale, blocks), out_shape...]
    pallas_call x1, Pallas kernels: 3.86 us -> 2.96 us  [mix(): pl.pallas_call(functools.partial(mix_kernel, groups_n), out_shape=(jax.Sh...]
where the time goes in v3:
time: 87.5 us; the launch traced here: 87.2 us
  blocking collectives  63.6 us (73%)
  Pallas kernels  13.6 us (16%)
  waiting for transfers between devices  6.67 us (8%)
  starting transfers between devices  1.76 us (2%)
    all_to_all x4, blocking collectives, all_to_all(): lax.all_to_all(value, 'grp', split_axis=0, concat_axis=0, tiled=True, axi...  54.1 us
    all_to_all x1, blocking collectives, on_device(): lax.all_to_all(small_gram(owned, groups_n, (devices, 1, groups_n * groups...  9.59 us
    ppermute x1, waiting for transfers between devices, on_device(): chunk = chunk + lax.ppermute(chunk, 'grp', across)  4.8 us
    pallas_call x1, Pallas kernels, finish(): pl.pallas_call(functools.partial(finish_kernel, scale, blocks), out_shape...  4.32 us
    pallas_call x1, Pallas kernels, project_first(): pl.pallas_call(first_kernel, in_specs=[pl.BlockSpec(memory_space=pl.ANY),...  2.99 us
    pallas_call x1, Pallas kernels, mix(): pl.pallas_call(functools.partial(mix_kernel, groups_n), out_shape=(jax.Sh...  2.96 us
  transfers between devices with their start and end apart: 4, of which 4 were waited for; matrix products, arithmetic and copies ran while one was open for 1% of the time, Pallas kernels for 2%

profile of v3, /device:TPU:0, one launch (start us, length us, event | category | flops | bytes accessed | tf_op | source)
XLA Modules:
  0.0 87.2 jit_solution(17268766049115255000)
XLA Ops:
  0.6 0.0 copy-start
  0.6 3.0 %project_first.1 = (f32[128,512]{1,0:T(8,128)S(1)}, bf16[1024,512]{1,0:T(8,128)(2,1)S(1)}, bf16[1024,512]{1,0:T(8,128)(2,1)S(1)}, f32[1024,512]{1,0:T(8,128)S(1)}, bf16[1024,256]{1,0:T(8,128)(2,1)S(1)}) custom-call(f32[1024,1024]{1,0:T(8,128)} %bitcast.18, f32[1024,128]{1,0:T(8,128)} %factor_ref.1), custom_call_target="tpu_custom_call" | custom-call | tf_op jit(solution)/shard_map/project_first/pallas_call | solution.py:137
  3.6 0.6 collective-permute-start
  4.2 0.7 project_second.1
  4.9 0.5 collective-permute-done
  5.4 18.2 %all_to_all.25 = f32[16,8,512]{2,1,0:T(8,128)S(1)} all-to-all(f32[16,8,512]{2,1,0:T(8,128)S(1)} %add_bitcast_fusion), channel_id=1, replica_groups=mesh['grp'=16,'rep'=2] {'grp'}, dimensions={0} | all-to-all | bytes 524288 | tf_op jit(solution)/shard_map/all_to_all | solution.py:347
  23.6 0.6 small_gram.1
  24.2 9.6 %all_to_all.26.gram_ref = f32[32,1,256]{2,1,0:T(1,128)S(1)} all-to-all(f32[32,1,256]{2,1,0:T(1,128)S(1)} %small_gram.1), channel_id=1, replica_groups=mesh['grp'=16,'rep'=2] {'grp','rep'}, dimensions={0} | all-to-all | bytes 65536 | tf_op jit(solution)/shard_map/all_to_all | solution.py:361
  33.8 0.0 copy-done
  33.8 3.0 %mix.1 = (f32[128,512]{1,0:T(8,128)S(1)}, f32[16,8]{1,0:T(8,128)S(1)}) custom-call(f32[32,1,256]{2,1,0:T(1,128)S(1)} %all_to_all.26.gram_ref, f32[8,16]{1,0:T(8,128)S(1)} %bitcast.17, f32[128,512]{1,0:T(8,128)S(1)} %bitcast.12), custom_call_target="tpu_custom_call" | custom-call | tf_op jit(solution)/shard_map/mix/pallas_call | solution.py:293
  36.7 13.0 %all_to_all.27 = f32[16,8,512]{2,1,0:T(8,128)S(1)} all-to-all(f32[16,8,512]{2,1,0:T(8,128)S(1)} %bitcast.16), channel_id=1, replica_groups=mesh['grp'=16,'rep'=2] {'grp'}, dimensions={0} | all-to-all | bytes 524288 | tf_op jit(solution)/shard_map/all_to_all | solution.py:347
  49.7 0.0 collective-permute-start.1
  49.7 0.7 multiply.2.refs_0_
  50.5 0.8 collective-permute-done.1.weight_ref
  51.3 0.7 multiply.3
  52.0 12.4 %all_to_all.28 = f32[8,128,128]{2,1,0:T(8,128)S(1)} all-to-all(f32[8,128,128]{2,1,0:T(8,128)S(1)} %bitcast.13), channel_id=1, replica_groups={{0,2,4,6,8,10,12,14},{16,18,20,22,24,26,28,30},{1,3,5,7,9,11,13,15},{17..., dimensions={0} | all-to-all | bytes 1048576 | tf_op jit(solution)/shard_map/all_to_all | solution.py:347
  64.4 1.1 %collective-permute-start.2 = (f32[128,128]{1,0:T(8,128)S(1)}, f32[128,128]{1,0:T(8,128)S(1)}, u32[]{:S(2)}, u32[]{:S(2)}) collective-permute-start(f32[128,128]{1,0:T(8,128)S(1)} %reduce_sum.9), channel_id=1, source_target_pairs={{0,16},{2,18},{4,20},{6,22},{8,24},{10,26},{12,28},{14,30},{16,0},... | collective-permute-start | bytes 196616 | tf_op jit(solution)/shard_map/ppermute | solution.py:376
  65.6 4.8 %collective-permute-done.2 = f32[128,128]{1,0:T(8,128)S(1)} collective-permute-done((f32[128,128]{1,0:T(8,128)S(1)}, f32[128,128]{1,0:T(8,128)S(1)}, u32[]{:S(2)}, u32[]{:S(2)}) %collective-permute-start.2) | collective-permute-done | bytes 65568 | tf_op jit(solution)/shard_map/ppermute | solution.py:376
  70.4 10.4 %all_to_all.29 = f32[8,128,128]{2,1,0:T(8,128)S(1)} all-to-all(f32[8,128,128]{2,1,0:T(8,128)S(1)} %reshape_tile.3), channel_id=1, replica_groups={{0,2,4,6,8,10,12,14},{16,18,20,22,24,26,28,30},{1,3,5,7,9,11,13,15},{17..., dimensions={0} | all-to-all | bytes 1048576 | tf_op jit(solution)/shard_map/all_to_all | solution.py:347
  80.9 0.6 row_gram.1.mine_ref
  81.5 0.1 collective-permute-start.3
  81.6 0.7 copy.5
  82.3 0.6 collective-permute-done.3.other_ref
  82.8 4.3 %finish.1 = f32[1024,128]{1,0:T(8,128)} custom-call(f32[1024,128]{1,0:T(8,128)S(1)} %bitcast.10, f32[128,128]{1,0:T(8,128)S(1)} %row_gram.1.mine_ref, f32[128,128]{1,0:T(8,128)S(1)} %collective-permute-done.3.other_ref), custom_call_target="tpu_custom_call" | custom-call | tf_op jit(solution)/shard_map/finish/pallas_call | solution.py:318
  (4 shorter events, 0.1 us)
Async XLA Ops:
  0.6 33.2 %copy-start = (f32[16,8]{0,1:T(8,128)S(1)}, f32[16,8]{0,1:T(8,128)}, u32[]{:S(2)}) copy-start(f32[16,8]{0,1:T(8,128)} %param.5) | copy-start | bytes 1540
  3.6 1.7 %collective-permute-start = (f32[128,512]{1,0:T(8,128)S(1)}, f32[128,512]{1,0:T(8,128)S(1)}, u32[]{:S(2)}, u32[]{:S(2)}) collective-permute-start(f32[128,512]{1,0:T(8,128)S(1)} %get-tuple-element.17), channel_id=1, source_target_pairs={{0,1},{1,0},{2,3},{3,2},{4,5},{5,4},{6,7},{7,6},{8,9},{9,8},{10,11... | collective-permute-start | bytes 786440 | tf_op jit(solution)/shard_map/ppermute | solution.py:355
  49.7 1.5 %collective-permute-start.1 = (f32[128,512]{1,0:T(8,128)S(1)}, f32[128,512]{1,0:T(8,128)S(1)}, u32[]{:S(2)}, u32[]{:S(2)}) collective-permute-start(f32[128,512]{1,0:T(8,128)S(1)} %bitcast.14), channel_id=1, source_target_pairs={{0,1},{1,0},{2,3},{3,2},{4,5},{5,4},{6,7},{7,6},{8,9},{9,8},{10,11... | collective-permute-start | bytes 786440 | tf_op jit(solution)/shard_map/ppermute | solution.py:372
  64.4 5.9 %collective-permute-start.2 = (f32[128,128]{1,0:T(8,128)S(1)}, f32[128,128]{1,0:T(8,128)S(1)}, u32[]{:S(2)}, u32[]{:S(2)}) collective-permute-start(f32[128,128]{1,0:T(8,128)S(1)} %reduce_sum.9), channel_id=1, source_target_pairs={{0,16},{2,18},{4,20},{6,22},{8,24},{10,26},{12,28},{14,30},{16,0},... | collective-permute-start | bytes 196616 | tf_op jit(solution)/shard_map/ppermute | solution.py:376
  81.5 1.3 %collective-permute-start.3 = (f32[128,128]{1,0:T(8,128)S(1)}, f32[128,128]{1,0:T(8,128)S(1)}, u32[]{:S(2)}, u32[]{:S(2)}) collective-permute-start(f32[128,128]{1,0:T(8,128)S(1)} %row_gram.1.mine_ref), channel_id=1, source_target_pairs={{0,1},{1,0},{2,3},{3,2},{4,5},{5,4},{6,7},{7,6},{8,9},{9,8},{10,11... | collective-permute-start | bytes 196616 | tf_op jit(solution)/shard_map/ppermute | solution.py:379

commit v4 on v3

--- a/solution.py
+++ b/solution.py
@@ -41,32 +41,39 @@
     return high, middle, (rest - middle.astype(F32)).astype(BF16)
 
 
-def left6(value):
-    high, middle, low = split3(value)
-    return jnp.concatenate([high, high, middle, high, middle, low], axis=1)
-
-
-def right6(value):
-    high, middle, low = split3(value)
-    return jnp.concatenate([high, middle, high, low, middle, high], axis=0)
-
-
-def times(right):
-    size = right.shape[0]
-    if size <= 16:
-        rows = [right[k : k + 1, :] for k in range(size)]
-
-        def apply(left):
-            terms = [left[:, k : k + 1] * rows[k] for k in range(size)]
-            while len(terms) > 1:
-                terms = [sum(terms[i : i + 2]) for i in range(0, len(terms), 2)]
-            return terms[0]
-
-        return apply
-    if size % 128 == 0:
-        stacked = right6(right)
-        return lambda left: fastdot(left6(left), stacked, ((1,), (0,)))
-    return lambda left: dot(left, right)
+def tree_sum(terms):
+    while len(terms) > 1:
+        terms = [sum(terms[i : i + 2]) for i in range(0, len(terms), 2)]
+    return terms[0]
+
+
+def small_step(squared, factor, unit):
+    size = unit.shape[0]
+    columns = [jnp.broadcast_to(squared[:, k : k + 1], unit.shape) for k in range(size)]
+    turn = 1.5 * unit - 0.5 * squared
+    turn_columns = [1.5 * unit[:, k : k + 1] - 0.5 * columns[k] for k in range(size)]
+    turn_squared = tree_sum([turn_columns[k] * turn[k : k + 1] for k in range(size)])
+    factor = tree_sum([turn_columns[k] * factor[k : k + 1] for k in range(size)])
+    return tree_sum([columns[k] * turn_squared[k : k + 1] for k in range(size)]), factor
+
+
+def step(squared, factor, unit):
+    if unit.shape[0] <= 16:
+        return small_step(squared, factor, unit)
+    turn = 1.5 * unit - 0.5 * squared
+    if unit.shape[0] % 128:
+        return dot(dot(squared, turn), turn), dot(factor, turn)
+    high, low = split(squared)
+    stacked = jnp.concatenate([high, low, high], axis=0)
+
+    def by_squared(left):
+        left_high, left_low = split(left)
+        return fastdot(jnp.concatenate([left_high, left_high, left_low], axis=1), stacked, ((1,), (0,)))
+
+    rank = unit.shape[0]
+    both = by_squared(jnp.concatenate([squared, factor], axis=0))
+    turn = 2.25 * unit - 1.5 * squared + 0.25 * both[:rank]
+    return by_squared(turn), 1.5 * factor - 0.5 * both[rank:]
 
 
 def orth_factor(gram):
@@ -75,11 +82,7 @@
     squared = gram * (1.0 / total)
     factor = unit * lax.rsqrt(total)
     for step_index in range(STEPS):
-        turn = 1.5 * unit - 0.5 * squared
-        by_turn = times(turn)
-        factor = by_turn(factor) if step_index else factor[:1, :1] * turn
-        if step_index < STEPS - 1:
-            squared = by_turn(by_turn(squared))
+        squared, factor = step(squared, factor, unit)
     return factor
 
 

time: 87.5 us -> 86.2 us (0.985)
  Pallas kernels: 13.6 us -> 12.3 us
where the time goes in v4:
time: 86.2 us; the launch traced here: 85.8 us
  blocking collectives  63.6 us (74%)
  Pallas kernels  12.3 us (14%)
  waiting for transfers between devices  6.67 us (8%)
  starting transfers between devices  1.76 us (2%)
    all_to_all x4, blocking collectives, all_to_all(): lax.all_to_all(value, 'grp', split_axis=0, concat_axis=0, tiled=True, axi...  54.1 us
    all_to_all x1, blocking collectives, on_device(): lax.all_to_all(small_gram(owned, groups_n, (devices, 1, groups_n * groups...  9.59 us
    ppermute x1, waiting for transfers between devices, on_device(): chunk = chunk + lax.ppermute(chunk, 'grp', across)  4.8 us
    pallas_call x1, Pallas kernels, finish(): pl.pallas_call(functools.partial(finish_kernel, scale, blocks), out_shape...  3.52 us
    pallas_call x1, Pallas kernels, project_first(): pl.pallas_call(first_kernel, in_specs=[pl.BlockSpec(memory_space=pl.ANY),...  2.99 us
    pallas_call x1, Pallas kernels, mix(): pl.pallas_call(functools.partial(mix_kernel, groups_n), out_shape=(jax.Sh...  2.42 us
  transfers between devices with their start and end apart: 4, of which 4 were waited for; matrix products, arithmetic and copies ran while one was open for 1% of the time, Pallas kernels for 2%

profile of v4, /device:TPU:0, one launch (start us, length us, event | category | flops | bytes accessed | tf_op | source)
XLA Modules:
  0.0 85.8 jit_solution(14156205981484843990)
XLA Ops:
  0.6 0.0 copy-start
  0.6 3.0 %project_first.1 = (f32[128,512]{1,0:T(8,128)S(1)}, bf16[1024,512]{1,0:T(8,128)(2,1)S(1)}, bf16[1024,512]{1,0:T(8,128)(2,1)S(1)}, f32[1024,512]{1,0:T(8,128)S(1)}, bf16[1024,256]{1,0:T(8,128)(2,1)S(1)}) custom-call(f32[1024,1024]{1,0:T(8,128)} %bitcast.18, f32[1024,128]{1,0:T(8,128)} %factor_ref.1), custom_call_target="tpu_custom_call" | custom-call | tf_op jit(solution)/shard_map/project_first/pallas_call | solution.py:140
  3.6 0.6 collective-permute-start
  4.2 0.7 project_second.1
  4.9 0.5 collective-permute-done
  5.4 18.2 %all_to_all.25 = f32[16,8,512]{2,1,0:T(8,128)S(1)} all-to-all(f32[16,8,512]{2,1,0:T(8,128)S(1)} %add_bitcast_fusion), channel_id=1, replica_groups=mesh['grp'=16,'rep'=2] {'grp'}, dimensions={0} | all-to-all | bytes 524288 | tf_op jit(solution)/shard_map/all_to_all | solution.py:350
  23.6 0.6 small_gram.1
  24.2 9.6 %all_to_all.26.gram_ref = f32[32,1,256]{2,1,0:T(1,128)S(1)} all-to-all(f32[32,1,256]{2,1,0:T(1,128)S(1)} %small_gram.1), channel_id=1, replica_groups=mesh['grp'=16,'rep'=2] {'grp','rep'}, dimensions={0} | all-to-all | bytes 65536 | tf_op jit(solution)/shard_map/all_to_all | solution.py:364
  33.8 0.0 copy-done
  33.8 2.4 %mix.1 = (f32[128,512]{1,0:T(8,128)S(1)}, f32[16,8]{1,0:T(8,128)S(1)}) custom-call(f32[32,1,256]{2,1,0:T(1,128)S(1)} %all_to_all.26.gram_ref, f32[8,16]{1,0:T(8,128)S(1)} %bitcast.17, f32[128,512]{1,0:T(8,128)S(1)} %bitcast.12), custom_call_target="tpu_custom_call" | custom-call | tf_op jit(solution)/shard_map/mix/pallas_call | solution.py:296
  36.2 13.0 %all_to_all.27 = f32[16,8,512]{2,1,0:T(8,128)S(1)} all-to-all(f32[16,8,512]{2,1,0:T(8,128)S(1)} %bitcast.16), channel_id=1, replica_groups=mesh['grp'=16,'rep'=2] {'grp'}, dimensions={0} | all-to-all | bytes 524288 | tf_op jit(solution)/shard_map/all_to_all | solution.py:350
  49.2 0.0 collective-permute-start.1
  49.2 0.7 multiply.2.refs_0_
  49.9 0.8 collective-permute-done.1.weight_ref
  50.8 0.7 multiply.3
  51.5 12.4 %all_to_all.28 = f32[8,128,128]{2,1,0:T(8,128)S(1)} all-to-all(f32[8,128,128]{2,1,0:T(8,128)S(1)} %bitcast.13), channel_id=1, replica_groups={{0,2,4,6,8,10,12,14},{16,18,20,22,24,26,28,30},{1,3,5,7,9,11,13,15},{17..., dimensions={0} | all-to-all | bytes 1048576 | tf_op jit(solution)/shard_map/all_to_all | solution.py:350
  63.9 1.1 %collective-permute-start.2 = (f32[128,128]{1,0:T(8,128)S(1)}, f32[128,128]{1,0:T(8,128)S(1)}, u32[]{:S(2)}, u32[]{:S(2)}) collective-permute-start(f32[128,128]{1,0:T(8,128)S(1)} %reduce_sum.9), channel_id=1, source_target_pairs={{0,16},{2,18},{4,20},{6,22},{8,24},{10,26},{12,28},{14,30},{16,0},... | collective-permute-start | bytes 196616 | tf_op jit(solution)/shard_map/ppermute | solution.py:379
  65.0 4.8 %collective-permute-done.2 = f32[128,128]{1,0:T(8,128)S(1)} collective-permute-done((f32[128,128]{1,0:T(8,128)S(1)}, f32[128,128]{1,0:T(8,128)S(1)}, u32[]{:S(2)}, u32[]{:S(2)}) %collective-permute-start.2) | collective-permute-done | bytes 65568 | tf_op jit(solution)/shard_map/ppermute | solution.py:379
  69.9 10.4 %all_to_all.29 = f32[8,128,128]{2,1,0:T(8,128)S(1)} all-to-all(f32[8,128,128]{2,1,0:T(8,128)S(1)} %reshape_tile.3), channel_id=1, replica_groups={{0,2,4,6,8,10,12,14},{16,18,20,22,24,26,28,30},{1,3,5,7,9,11,13,15},{17..., dimensions={0} | all-to-all | bytes 1048576 | tf_op jit(solution)/shard_map/all_to_all | solution.py:350
  80.3 0.6 row_gram.1.mine_ref
  81.0 0.1 collective-permute-start.3
  81.1 0.7 copy.5
  81.7 0.6 collective-permute-done.3.other_ref
  82.3 3.5 %finish.1 = f32[1024,128]{1,0:T(8,128)} custom-call(f32[1024,128]{1,0:T(8,128)S(1)} %bitcast.10, f32[128,128]{1,0:T(8,128)S(1)} %row_gram.1.mine_ref, f32[128,128]{1,0:T(8,128)S(1)} %collective-permute-done.3.other_ref), custom_call_target="tpu_custom_call" | custom-call | tf_op jit(solution)/shard_map/finish/pallas_call | solution.py:321
  (4 shorter events, 0.1 us)
Async XLA Ops:
  0.6 33.2 %copy-start = (f32[16,8]{0,1:T(8,128)S(1)}, f32[16,8]{0,1:T(8,128)}, u32[]{:S(2)}) copy-start(f32[16,8]{0,1:T(8,128)} %param.5) | copy-start | bytes 1540
  3.6 1.7 %collective-permute-start = (f32[128,512]{1,0:T(8,128)S(1)}, f32[128,512]{1,0:T(8,128)S(1)}, u32[]{:S(2)}, u32[]{:S(2)}) collective-permute-start(f32[128,512]{1,0:T(8,128)S(1)} %get-tuple-element.17), channel_id=1, source_target_pairs={{0,1},{1,0},{2,3},{3,2},{4,5},{5,4},{6,7},{7,6},{8,9},{9,8},{10,11... | collective-permute-start | bytes 786440 | tf_op jit(solution)/shard_map/ppermute | solution.py:358
  49.2 1.5 %collective-permute-start.1 = (f32[128,512]{1,0:T(8,128)S(1)}, f32[128,512]{1,0:T(8,128)S(1)}, u32[]{:S(2)}, u32[]{:S(2)}) collective-permute-start(f32[128,512]{1,0:T(8,128)S(1)} %bitcast.14), channel_id=1, source_target_pairs={{0,1},{1,0},{2,3},{3,2},{4,5},{5,4},{6,7},{7,6},{8,9},{9,8},{10,11... | collective-permute-start | bytes 786440 | tf_op jit(solution)/shard_map/ppermute | solution.py:375
  63.9 5.9 %collective-permute-start.2 = (f32[128,128]{1,0:T(8,128)S(1)}, f32[128,128]{1,0:T(8,128)S(1)}, u32[]{:S(2)}, u32[]{:S(2)}) collective-permute-start(f32[128,128]{1,0:T(8,128)S(1)} %reduce_sum.9), channel_id=1, source_target_pairs={{0,16},{2,18},{4,20},{6,22},{8,24},{10,26},{12,28},{14,30},{16,0},... | collective-permute-start | bytes 196616 | tf_op jit(solution)/shard_map/ppermute | solution.py:379
  81.0 1.3 %collective-permute-start.3 = (f32[128,128]{1,0:T(8,128)S(1)}, f32[128,128]{1,0:T(8,128)S(1)}, u32[]{:S(2)}, u32[]{:S(2)}) collective-permute-start(f32[128,128]{1,0:T(8,128)S(1)} %row_gram.1.mine_ref), channel_id=1, source_target_pairs={{0,1},{1,0},{2,3},{3,2},{4,5},{5,4},{6,7},{7,6},{8,9},{9,8},{10,11... | collective-permute-start | bytes 196616 | tf_op jit(solution)/shard_map/ppermute | solution.py:382

commit v5 on v4

--- a/solution.py
+++ b/solution.py
@@ -91,66 +91,76 @@
     return jnp.concatenate([high, low], axis=1)
 
 
+def packed_shape(groups_n, cuts, rank, width):
+    return (rank, width) if cuts == 1 else (groups_n, cuts, rank // groups_n, width // cuts)
+
+
+def store(ref, value, add=False):
+    if len(ref.shape) == 2:
+        ref[...] = ref[...] + value if add else value
+        return
+    groups_n, cuts, per, piece = ref.shape
+    for k in range(cuts):
+        part = value[:, k * piece : (k + 1) * piece].reshape(groups_n, per, piece)
+        ref[:, k] = ref[:, k] + part if add else part
+
+
+def load(ref):
+    if len(ref.shape) == 2:
+        return ref[...]
+    groups_n, cuts, per, piece = ref.shape
+    return jnp.concatenate([ref[:, k].reshape(groups_n * per, piece) for k in range(cuts)], axis=1)
+
+
 def project_block(image_high, image_low, factor_both):
     rank = factor_both.shape[1] // 2
     wide = fastdot(factor_both, image_high, ((0,), (0,)))
     return wide[:rank] + wide[rank:] + fastdot(factor_both[:, :rank], image_low, ((0,), (0,)))
 
 
-def first_kernel(
-    image_ref, factor_ref, out_ref, high_ref, low_ref, later_ref, both_ref, now_ref, fetched_ref, image_sems, factor_sem
-):
-    parts, blocks = image_sems.shape
-    rows, width = now_ref.shape
+def columns_of(part, width):
+    return pl.ds(pl.multiple_of(lax.rem(lax.axis_index("rep") + part, lax.axis_size("rep")) * width, width), width)
+
+
+def first_kernel(image_ref, factor_ref, out_ref, high_ref, low_ref, held_ref, both_ref, fetched_ref, sems, factor_sem):
+    blocks = sems.shape[0]
+    rows, width = high_ref.shape
     block = rows // blocks
-    me = lax.axis_index("rep")
+    copies = []
     factor_copy = pltpu.make_async_copy(factor_ref, fetched_ref, factor_sem)
     factor_copy.start()
-    copies = []
-    for part, held_ref in enumerate((now_ref, later_ref)):
-        at = pl.multiple_of(lax.rem(me + 1 + part, parts) * width, width)
-        for i in range(blocks):
-            take = pl.ds(i * block, block)
-            copy = pltpu.make_async_copy(image_ref.at[take, pl.ds(at, width)], held_ref.at[take], image_sems.at[part, i])
-            copies.append(copy)
-    for copy in copies[:blocks]:
-        copy.start()
+    for i in range(blocks):
+        take = pl.ds(i * block, block)
+        copies.append(pltpu.make_async_copy(image_ref.at[take], held_ref.at[take], sems.at[i]))
+        copies[-1].start()
     factor_copy.wait()
     both_ref[...] = halves_of(fetched_ref[...])
+    columns = columns_of(1, width)
     for i in range(blocks):
         copies[i].wait()
-        copies[blocks + i].start()
         take = pl.ds(i * block, block)
-        high, low = split(now_ref[take])
+        high, low = split(held_ref[take, columns])
         high_ref[take] = high
         low_ref[take] = low
         value = project_block(high, low, both_ref[take])
-        if i == 0:
-            out_ref[...] = value
-        else:
-            out_ref[...] += value
-    for copy in copies[blocks:]:
-        copy.wait()
-
-
-def project_first(image, row_factor, width, blocks=4):
-    rows = image.shape[0]
-    rank = row_factor.shape[1]
-    parts = image.shape[1] // width
+        store(out_ref, value, add=i > 0)
+
+
+def project_first(image, row_factor, width, packed, blocks=2):
+    rows, rank = row_factor.shape
     return pl.pallas_call(
         first_kernel,
         in_specs=[pl.BlockSpec(memory_space=pl.ANY), pl.BlockSpec(memory_space=pl.ANY)],
         out_shape=(
-            jax.ShapeDtypeStruct((rank, width), F32),
+            jax.ShapeDtypeStruct(packed, F32),
             jax.ShapeDtypeStruct((rows, width), BF16),
             jax.ShapeDtypeStruct((rows, width), BF16),
-            jax.ShapeDtypeStruct((rows, width), F32),
+            jax.ShapeDtypeStruct(image.shape, F32),
             jax.ShapeDtypeStruct((rows, 2 * rank), BF16),
         ),
         scratch_shapes=[
-            pltpu.VMEM((rows, width), F32),
             pltpu.VMEM((rows, rank), F32),
-            pltpu.SemaphoreType.DMA((parts, blocks)),
+            pltpu.SemaphoreType.DMA((blocks,)),
             pltpu.SemaphoreType.DMA,
         ],
         compiler_params=SMALL,
@@ -161,26 +171,27 @@
     )
 
 
-def second_kernel(blocks, image_ref, both_ref, out_ref, high_ref, low_ref):
-    block = image_ref.shape[0] // blocks
+def second_kernel(blocks, held_ref, both_ref, out_ref, high_ref, low_ref):
+    rows, width = high_ref.shape
+    block = rows // blocks
+    columns = columns_of(0, width)
     total = None
     for i in range(blocks):
         take = pl.ds(i * block, block)
-        high, low = split(image_ref[take])
+        high, low = split(held_ref[take, columns])
         high_ref[take] = high
         low_ref[take] = low
         value = project_block(high, low, both_ref[take])
         total = value if total is None else total + value
-    out_ref[...] = total
-
-
-def project_second(image, both, blocks=4):
-    rows, width = image.shape
-    rank = both.shape[1] // 2
+    store(out_ref, total)
+
+
+def project_second(held, both, width, packed, blocks=4):
+    rows, rank = both.shape[0], both.shape[1] // 2
     return pl.pallas_call(
         functools.partial(second_kernel, blocks),
         out_shape=(
-            jax.ShapeDtypeStruct((rank, width), F32),
+            jax.ShapeDtypeStruct(packed, F32),
             jax.ShapeDtypeStruct((rows, width), BF16),
             jax.ShapeDtypeStruct((rows, width), BF16),
         ),
@@ -189,12 +200,12 @@
         ),
         compiler_params=SMALL,
         name="project_second",
-    )(image, both)
+    )(held, both)
 
 
 def product_kernel(blocks, high_ref, low_ref, weight_ref, *refs):
     out_ref = refs[-1]
-    weight_high, weight_low = split(weight_ref[...])
+    weight_high, weight_low = split(load(weight_ref))
     rank = weight_high.shape[0]
     both = jnp.concatenate([weight_high, weight_low], axis=0)
     block = out_ref.shape[0] // blocks
@@ -209,7 +220,7 @@
 
 def multiply(high, low, weight, start=None, blocks=4):
     rows, width = high.shape
-    rank = weight.shape[0]
+    rank = weight.size // width
     more = () if start is None else (start,)
     return pl.pallas_call(
         functools.partial(product_kernel, blocks),
@@ -238,10 +249,12 @@
 
 
 def gram_kernel(groups_n, owned_ref, out_ref):
-    owned = owned_ref[...]
-    rank = owned.shape[0]
+    high, low = split(load(owned_ref))
+    rank = high.shape[0]
     per = rank // groups_n
-    full = jnp.where(same_slot(groups_n, rank), dot(owned, owned, ((1,), (1,))), 0.0)
+    wide = fastdot(high, jnp.concatenate([high, low], axis=0), ((1,), (1,)))
+    full = wide[:, :rank] + wide[:, rank:] + wide[:, rank:].T
+    full = jnp.where(same_slot(groups_n, rank), full, 0.0)
     if len(out_ref.shape) == 2:
         fold = spread(groups_n, rank)
         out_ref[...] = dot(dot(fold, full, ((0,), (0,))), fold)
@@ -266,7 +279,8 @@
 
 
 def mix_kernel(groups_n, gram_ref, time_ref, owned_ref, out_ref, time_out_ref):
-    rank = owned_ref.shape[0]
+    owned_high, owned_low = split(load(owned_ref))
+    rank = owned_high.shape[0]
     per = rank // groups_n
     if len(gram_ref.shape) == 2:
         fold = spread(groups_n, rank)
@@ -282,12 +296,12 @@
     basis = dot(start, orth_factor(dot(turned, start) * (1.0 / per)))
     mixer = jnp.where(same_slot(groups_n, rank), dot(basis, basis, ((1,), (1,))), 0.0)
     mixer_high, mixer_low = split(mixer)
-    owned_high, owned_low = split(owned_ref[...])
-    out_ref[...] = fastdot(
+    mixed = fastdot(
         jnp.concatenate([mixer_high, mixer_low, mixer_high], axis=1),
         jnp.concatenate([owned_high, owned_high, owned_low], axis=0),
         ((1,), (0,)),
     )
+    store(out_ref, mixed)
     one_of_each = cells(groups_n, rank, lambda row: row * per, lambda cell: cell)
     time_out_ref[...] = dot(one_of_each, basis) * math.sqrt(groups_n)
 
@@ -329,8 +343,10 @@
 
 
 def row_gram_kernel(block_ref, out_ref):
-    block = block_ref[...]
-    out_ref[...] = dot(block, block, ((0,), (0,)))
+    high, low = split(block_ref[...])
+    rank = high.shape[1]
+    wide = fastdot(high, jnp.concatenate([high, low], axis=1), ((0,), (0,)))
+    out_ref[...] = wide[:, :rank] + wide[:, rank:] + wide[:, rank:].T
 
 
 def row_gram(block):
@@ -350,15 +366,23 @@
         value = lax.all_to_all(value, "grp", split_axis=0, concat_axis=0, tiled=True, axis_index_groups=groups)
         return value.reshape(shape)
 
+    def to_owners(value):
+        if len(value.shape) == 2:
+            return all_to_all(value, groups_n)
+        flat = value.reshape((groups_n * reps,) + value.shape[2:])
+        return lax.all_to_all(flat, ("grp", "rep"), split_axis=0, concat_axis=0, tiled=True).reshape(value.shape)
+
     def on_device(snapshots, row_factor, time_factor):
         rows, cols = snapshots.shape[1:]
         rank = row_factor.shape[1]
         width = cols // reps
-        send, far_high, far_low, near, both = project_first(snapshots[0], row_factor, width)
+        fits = rank % (8 * groups_n) == 0 and width % (128 * reps) == 0
+        packed = packed_shape(groups_n, reps if fits else 1, rank, width)
+        send, far_high, far_low, held, both = project_first(snapshots[0], row_factor, width, packed)
         received = lax.ppermute(send, "rep", swap)
-        summed, near_high, near_low = project_second(near, both)
+        summed, near_high, near_low = project_second(held, both, width, packed)
         summed = summed + received
-        owned = all_to_all(summed, groups_n)
+        owned = to_owners(summed)
         devices = groups_n * reps
         if devices * groups_n * groups_n <= 1 << 20:
             grams = lax.all_to_all(
@@ -371,7 +395,7 @@
         else:
             grams = lax.psum(small_gram(owned, groups_n, (groups_n, groups_n)), ("grp", "rep"))
         weights, new_time = mix(grams, time_factor, owned, groups_n)
-        weight = all_to_all(weights, groups_n)
+        weight = to_owners(weights)
         other_weight = lax.ppermute(weight, "rep", swap)
         product = multiply(far_high, far_low, other_weight, multiply(near_high, near_low, weight))
         parts = all_to_all(product, half_n, halves)

time: 86.2 us -> 84.1 us (0.976)
  blocking collectives: 63.6 us -> 62.2 us
    all_to_all x4 -> x2, blocking collectives: 54.1 us -> 22.9 us  [all_to_all(): lax.all_to_all(value, 'grp', split_axis=0, concat_axis=0, tiled=True, axi...]
    all_to_all x0 -> x2, blocking collectives: none -> 29.9 us  [to_owners(): lax.all_to_all(flat, ('grp', 'rep'), split_axis=0, concat_axis=0, tiled=T...]
where the time goes in v5:
time: 84.1 us; the launch traced here: 83.8 us
  blocking collectives  62.2 us (74%)
  Pallas kernels  11.8 us (14%)
  waiting for transfers between devices  6.84 us (8%)
  starting transfers between devices  1.58 us (2%)
    all_to_all x2, blocking collectives, to_owners(): lax.all_to_all(flat, ('grp', 'rep'), split_axis=0, concat_axis=0, tiled=T...  29.9 us
    all_to_all x2, blocking collectives, all_to_all(): lax.all_to_all(value, 'grp', split_axis=0, concat_axis=0, tiled=True, axi...  22.9 us
    all_to_all x1, blocking collectives, on_device(): lax.all_to_all(small_gram(owned, groups_n, (devices, 1, groups_n * groups...  9.46 us
    ppermute x1, waiting for transfers between devices, on_device(): chunk = chunk + lax.ppermute(chunk, 'grp', across)  4.98 us
    pallas_call x1, Pallas kernels, finish(): pl.pallas_call(functools.partial(finish_kernel, scale, blocks), out_shape...  3.52 us
    pallas_call x1, Pallas kernels, project_first(): pl.pallas_call(first_kernel, in_specs=[pl.BlockSpec(memory_space=pl.ANY),...  2.83 us
    pallas_call x1, Pallas kernels, mix(): pl.pallas_call(functools.partial(mix_kernel, groups_n), out_shape=(jax.Sh...  2.42 us
  transfers between devices with their start and end apart: 4, of which 4 were waited for; matrix products, arithmetic and copies ran while one was open for 1% of the time, Pallas kernels for 2%

profile of v5, /device:TPU:0, one launch (start us, length us, event | category | flops | bytes accessed | tf_op | source)
XLA Modules:
  0.0 83.8 jit_solution(9098520977141046976)
XLA Ops:
  0.6 2.8 %project_first.1 = (f32[16,2,8,256]{3,2,1,0:T(8,128)S(1)}, bf16[1024,512]{1,0:T(8,128)(2,1)S(1)}, bf16[1024,512]{1,0:T(8,128)(2,1)S(1)}, f32[1024,1024]{1,0:T(8,128)S(1)}, bf16[1024,256]{1,0:T(8,128)(2,1)S(1)}) custom-call(f32[1024,1024]{1,0:T(8,128)} %bitcast.17, f32[1024,128]{1,0:T(8,128)} %factor_ref.1), custom_call_target="tpu_custom_call" | custom-call | tf_op jit(solution)/shard_map/project_first/pallas_call | solution.py:151
  3.5 0.0 copy-start
  3.5 0.6 collective-permute-start
  4.0 0.7 project_second.1
  4.7 0.5 collective-permute-done
  5.2 17.6 %all_to_all.25 = f32[32,8,256]{2,1,0:T(8,128)S(1)} all-to-all(f32[32,8,256]{2,1,0:T(8,128)S(1)} %bitcast.18), channel_id=1, replica_groups=mesh['grp'=16,'rep'=2] {'grp','rep'}, dimensions={0} | all-to-all | bytes 524288 | tf_op jit(solution)/shard_map/all_to_all | solution.py:373
  22.8 0.5 small_gram.1
  23.4 9.5 %all_to_all.26.gram_ref = f32[32,1,256]{2,1,0:T(1,128)S(1)} all-to-all(f32[32,1,256]{2,1,0:T(1,128)S(1)} %small_gram.1), channel_id=1, replica_groups=mesh['grp'=16,'rep'=2] {'grp','rep'}, dimensions={0} | all-to-all | bytes 65536 | tf_op jit(solution)/shard_map/all_to_all | solution.py:388
  32.8 0.0 copy-done
  32.8 2.4 %mix.1 = (f32[16,2,8,256]{3,2,1,0:T(8,128)S(1)}, f32[16,8]{1,0:T(8,128)S(1)}) custom-call(f32[32,1,256]{2,1,0:T(1,128)S(1)} %all_to_all.26.gram_ref, f32[8,16]{1,0:T(8,128)S(1)} %bitcast.16, f32[16,2,8,256]{3,2,1,0:T(8,128)S(1)} %bitcast.11), custom_call_target="tpu_custom_call" | custom-call | tf_op jit(solution)/shard_map/mix/pallas_call | solution.py:310
  35.3 12.3 %all_to_all.27 = f32[32,8,256]{2,1,0:T(8,128)S(1)} all-to-all(f32[32,8,256]{2,1,0:T(8,128)S(1)} %bitcast.15), channel_id=1, replica_groups=mesh['grp'=16,'rep'=2] {'grp','rep'}, dimensions={0} | all-to-all | bytes 524288 | tf_op jit(solution)/shard_map/all_to_all | solution.py:373
  47.5 0.0 collective-permute-start.1
  47.5 0.7 multiply.2.refs_0_
  48.3 0.8 collective-permute-done.1.weight_ref
  49.1 0.7 multiply.3
  49.8 12.4 %all_to_all.28 = f32[8,128,128]{2,1,0:T(8,128)S(1)} all-to-all(f32[8,128,128]{2,1,0:T(8,128)S(1)} %bitcast.12), channel_id=1, replica_groups={{0,2,4,6,8,10,12,14},{16,18,20,22,24,26,28,30},{1,3,5,7,9,11,13,15},{17..., dimensions={0} | all-to-all | bytes 1048576 | tf_op jit(solution)/shard_map/all_to_all | solution.py:366
  62.2 0.9 %collective-permute-start.2 = (f32[128,128]{1,0:T(8,128)S(1)}, f32[128,128]{1,0:T(8,128)S(1)}, u32[]{:S(2)}, u32[]{:S(2)}) collective-permute-start(f32[128,128]{1,0:T(8,128)S(1)} %reduce_sum.9), channel_id=1, source_target_pairs={{0,16},{2,18},{4,20},{6,22},{8,24},{10,26},{12,28},{14,30},{16,0},... | collective-permute-start | bytes 196616 | tf_op jit(solution)/shard_map/ppermute | solution.py:403
  63.2 5.0 %collective-permute-done.2 = f32[128,128]{1,0:T(8,128)S(1)} collective-permute-done((f32[128,128]{1,0:T(8,128)S(1)}, f32[128,128]{1,0:T(8,128)S(1)}, u32[]{:S(2)}, u32[]{:S(2)}) %collective-permute-start.2) | collective-permute-done | bytes 65568 | tf_op jit(solution)/shard_map/ppermute | solution.py:403
  68.2 10.4 %all_to_all.29 = f32[8,128,128]{2,1,0:T(8,128)S(1)} all-to-all(f32[8,128,128]{2,1,0:T(8,128)S(1)} %reshape_tile.3), channel_id=1, replica_groups={{0,2,4,6,8,10,12,14},{16,18,20,22,24,26,28,30},{1,3,5,7,9,11,13,15},{17..., dimensions={0} | all-to-all | bytes 1048576 | tf_op jit(solution)/shard_map/all_to_all | solution.py:366
  78.7 0.3 row_gram.1.mine_ref
  79.0 0.1 collective-permute-start.3
  79.1 0.7 copy.5
  79.7 0.6 collective-permute-done.3.other_ref
  80.3 3.5 %finish.1 = f32[1024,128]{1,0:T(8,128)} custom-call(f32[1024,128]{1,0:T(8,128)S(1)} %bitcast.9, f32[128,128]{1,0:T(8,128)S(1)} %row_gram.1.mine_ref, f32[128,128]{1,0:T(8,128)S(1)} %collective-permute-done.3.other_ref), custom_call_target="tpu_custom_call" | custom-call | tf_op jit(solution)/shard_map/finish/pallas_call | solution.py:335
  (4 shorter events, 0.1 us)
Async XLA Ops:
  3.5 29.4 %copy-start = (f32[16,8]{0,1:T(8,128)S(1)}, f32[16,8]{0,1:T(8,128)}, u32[]{:S(2)}) copy-start(f32[16,8]{0,1:T(8,128)} %param.5) | copy-start | bytes 1540
  3.5 1.7 %collective-permute-start = (f32[16,2,8,256]{3,2,1,0:T(8,128)S(1)}, f32[16,2,8,256]{3,2,1,0:T(8,128)S(1)}, u32[]{:S(2)}, u32[]{:S(2)}) collective-permute-start(f32[16,2,8,256]{3,2,1,0:T(8,128)S(1)} %get-tuple-element.17), channel_id=1, source_target_pairs={{0,1},{1,0},{2,3},{3,2},{4,5},{5,4},{6,7},{7,6},{8,9},{9,8},{10,11... | collective-permute-start | bytes 786440 | tf_op jit(solution)/shard_map/ppermute | solution.py:382
  47.5 1.5 %collective-permute-start.1 = (f32[16,2,8,256]{3,2,1,0:T(8,128)S(1)}, f32[16,2,8,256]{3,2,1,0:T(8,128)S(1)}, u32[]{:S(2)}, u32[]{:S(2)}) collective-permute-start(f32[16,2,8,256]{3,2,1,0:T(8,128)S(1)} %bitcast.13), channel_id=1, source_target_pairs={{0,1},{1,0},{2,3},{3,2},{4,5},{5,4},{6,7},{7,6},{8,9},{9,8},{10,11... | collective-permute-start | bytes 786440 | tf_op jit(solution)/shard_map/ppermute | solution.py:399
  62.2 5.9 %collective-permute-start.2 = (f32[128,128]{1,0:T(8,128)S(1)}, f32[128,128]{1,0:T(8,128)S(1)}, u32[]{:S(2)}, u32[]{:S(2)}) collective-permute-start(f32[128,128]{1,0:T(8,128)S(1)} %reduce_sum.9), channel_id=1, source_target_pairs={{0,16},{2,18},{4,20},{6,22},{8,24},{10,26},{12,28},{14,30},{16,0},... | collective-permute-start | bytes 196616 | tf_op jit(solution)/shard_map/ppermute | solution.py:403
  79.0 1.3 %collective-permute-start.3 = (f32[128,128]{1,0:T(8,128)S(1)}, f32[128,128]{1,0:T(8,128)S(1)}, u32[]{:S(2)}, u32[]{:S(2)}) collective-permute-start(f32[128,128]{1,0:T(8,128)S(1)} %row_gram.1.mine_ref), channel_id=1, source_target_pairs={{0,1},{1,0},{2,3},{3,2},{4,5},{5,4},{6,7},{7,6},{8,9},{9,8},{10,11... | collective-permute-start | bytes 196616 | tf_op jit(solution)/shard_map/ppermute | solution.py:406

commit v6 on v5

--- a/solution.py
+++ b/solution.py
@@ -39,6 +39,22 @@
     rest = value - high.astype(F32)
     middle = rest.astype(BF16)
     return high, middle, (rest - middle.astype(F32)).astype(BF16)
+
+
+def halves_of(value):
+    high, low = split(value)
+    return jnp.concatenate([high, low], axis=1)
+
+
+def stack(right):
+    both = halves_of(right)
+    return jnp.concatenate([both, both], axis=0)
+
+
+def by_stacked(left_halves, stacked):
+    wide = fastdot(left_halves, stacked, ((1,), (0,)))
+    size = stacked.shape[1] // 2
+    return wide[:, :size] + wide[:, size:]
 
 
 def tree_sum(terms):
@@ -63,17 +79,11 @@
     turn = 1.5 * unit - 0.5 * squared
     if unit.shape[0] % 128:
         return dot(dot(squared, turn), turn), dot(factor, turn)
-    high, low = split(squared)
-    stacked = jnp.concatenate([high, low, high], axis=0)
-
-    def by_squared(left):
-        left_high, left_low = split(left)
-        return fastdot(jnp.concatenate([left_high, left_high, left_low], axis=1), stacked, ((1,), (0,)))
-
     rank = unit.shape[0]
-    both = by_squared(jnp.concatenate([squared, factor], axis=0))
+    stacked = stack(squared)
+    both = by_stacked(halves_of(jnp.concatenate([squared, factor], axis=0)), stacked)
     turn = 2.25 * unit - 1.5 * squared + 0.25 * both[:rank]
-    return by_squared(turn), 1.5 * factor - 0.5 * both[rank:]
+    return by_stacked(halves_of(turn), stacked), 1.5 * factor - 0.5 * both[rank:]
 
 
 def orth_factor(gram):
@@ -84,11 +94,6 @@
     for step_index in range(STEPS):
         squared, factor = step(squared, factor, unit)
     return factor
-
-
-def halves_of(value):
-    high, low = split(value)
-    return jnp.concatenate([high, low], axis=1)
 
 
 def packed_shape(groups_n, cuts, rank, width):
@@ -317,14 +322,12 @@
 
 def finish_kernel(scale, blocks, block_ref, mine_ref, other_ref, out_ref, made_ref, sems):
     rows = block_ref.shape[0] // blocks
-    high, low = split(block_ref[...])
-    left = jnp.concatenate([high, low, high], axis=1)
-    factor_high, factor_low = split(orth_factor(mine_ref[...] + other_ref[...]) * scale)
-    right = jnp.concatenate([factor_high, factor_high, factor_low], axis=0)
+    left = halves_of(block_ref[...])
+    right = stack(orth_factor(mine_ref[...] + other_ref[...]) * scale)
     copies = []
     for i in range(blocks):
         take = pl.ds(i * rows, rows)
-        made_ref[take] = fastdot(left[i * rows : (i + 1) * rows], right, ((1,), (0,)))
+        made_ref[take] = by_stacked(left[i * rows : (i + 1) * rows], right)
         copies.append(pltpu.make_async_copy(made_ref.at[take], out_ref.at[take], sems.at[i]))
         copies[-1].start()
     for copy in copies:

time: 84.1 us -> 84.1 us (level)
  no operation moved by 1% of the time
where the time goes in v6:
time: 84.1 us; the launch traced here: 83.8 us
  blocking collectives  62.2 us (74%)
  Pallas kernels  11.8 us (14%)
  waiting for transfers between devices  6.84 us (8%)
  starting transfers between devices  1.58 us (2%)
    all_to_all x2, blocking collectives, to_owners(): lax.all_to_all(flat, ('grp', 'rep'), split_axis=0, concat_axis=0, tiled=T...  29.9 us
    all_to_all x2, blocking collectives, all_to_all(): lax.all_to_all(value, 'grp', split_axis=0, concat_axis=0, tiled=True, axi...  22.9 us
    all_to_all x1, blocking collectives, on_device(): lax.all_to_all(small_gram(owned, groups_n, (devices, 1, groups_n * groups...  9.46 us
    ppermute x1, waiting for transfers between devices, on_device(): chunk = chunk + lax.ppermute(chunk, 'grp', across)  4.98 us
    pallas_call x1, Pallas kernels, finish(): pl.pallas_call(functools.partial(finish_kernel, scale, blocks), out_shape...  3.51 us
    pallas_call x1, Pallas kernels, project_first(): pl.pallas_call(first_kernel, in_specs=[pl.BlockSpec(memory_space=pl.ANY),...  2.83 us
    pallas_call x1, Pallas kernels, mix(): pl.pallas_call(functools.partial(mix_kernel, groups_n), out_shape=(jax.Sh...  2.42 us
  transfers between devices with their start and end apart: 4, of which 4 were waited for; matrix products, arithmetic and copies ran while one was open for 1% of the time, Pallas kernels for 2%

profile of v6, /device:TPU:0, one launch (start us, length us, event | category | flops | bytes accessed | tf_op | source)
XLA Modules:
  0.0 83.8 jit_solution(1448018166342992463)
XLA Ops:
  0.6 2.8 %project_first.1 = (f32[16,2,8,256]{3,2,1,0:T(8,128)S(1)}, bf16[1024,512]{1,0:T(8,128)(2,1)S(1)}, bf16[1024,512]{1,0:T(8,128)(2,1)S(1)}, f32[1024,1024]{1,0:T(8,128)S(1)}, bf16[1024,256]{1,0:T(8,128)(2,1)S(1)}) custom-call(f32[1024,1024]{1,0:T(8,128)} %bitcast.17, f32[1024,128]{1,0:T(8,128)} %factor_ref.1), custom_call_target="tpu_custom_call" | custom-call | tf_op jit(solution)/shard_map/project_first/pallas_call | solution.py:156
  3.5 0.0 copy-start
  3.5 0.6 collective-permute-start
  4.0 0.7 project_second.1
  4.7 0.5 collective-permute-done
  5.2 17.6 %all_to_all.25 = f32[32,8,256]{2,1,0:T(8,128)S(1)} all-to-all(f32[32,8,256]{2,1,0:T(8,128)S(1)} %bitcast.18), channel_id=1, replica_groups=mesh['grp'=16,'rep'=2] {'grp','rep'}, dimensions={0} | all-to-all | bytes 524288 | tf_op jit(solution)/shard_map/all_to_all | solution.py:376
  22.8 0.5 small_gram.1
  23.4 9.5 %all_to_all.26.gram_ref = f32[32,1,256]{2,1,0:T(1,128)S(1)} all-to-all(f32[32,1,256]{2,1,0:T(1,128)S(1)} %small_gram.1), channel_id=1, replica_groups=mesh['grp'=16,'rep'=2] {'grp','rep'}, dimensions={0} | all-to-all | bytes 65536 | tf_op jit(solution)/shard_map/all_to_all | solution.py:391
  32.8 0.0 copy-done
  32.8 2.4 %mix.1 = (f32[16,2,8,256]{3,2,1,0:T(8,128)S(1)}, f32[16,8]{1,0:T(8,128)S(1)}) custom-call(f32[32,1,256]{2,1,0:T(1,128)S(1)} %all_to_all.26.gram_ref, f32[8,16]{1,0:T(8,128)S(1)} %bitcast.16, f32[16,2,8,256]{3,2,1,0:T(8,128)S(1)} %bitcast.11), custom_call_target="tpu_custom_call" | custom-call | tf_op jit(solution)/shard_map/mix/pallas_call | solution.py:315
  35.3 12.3 %all_to_all.27 = f32[32,8,256]{2,1,0:T(8,128)S(1)} all-to-all(f32[32,8,256]{2,1,0:T(8,128)S(1)} %bitcast.15), channel_id=1, replica_groups=mesh['grp'=16,'rep'=2] {'grp','rep'}, dimensions={0} | all-to-all | bytes 524288 | tf_op jit(solution)/shard_map/all_to_all | solution.py:376
  47.5 0.0 collective-permute-start.1
  47.5 0.7 multiply.2.refs_0_
  48.3 0.8 collective-permute-done.1.weight_ref
  49.1 0.7 multiply.3
  49.8 12.4 %all_to_all.28 = f32[8,128,128]{2,1,0:T(8,128)S(1)} all-to-all(f32[8,128,128]{2,1,0:T(8,128)S(1)} %bitcast.12), channel_id=1, replica_groups={{0,2,4,6,8,10,12,14},{16,18,20,22,24,26,28,30},{1,3,5,7,9,11,13,15},{17..., dimensions={0} | all-to-all | bytes 1048576 | tf_op jit(solution)/shard_map/all_to_all | solution.py:369
  62.2 0.9 %collective-permute-start.2 = (f32[128,128]{1,0:T(8,128)S(1)}, f32[128,128]{1,0:T(8,128)S(1)}, u32[]{:S(2)}, u32[]{:S(2)}) collective-permute-start(f32[128,128]{1,0:T(8,128)S(1)} %reduce_sum.9), channel_id=1, source_target_pairs={{0,16},{2,18},{4,20},{6,22},{8,24},{10,26},{12,28},{14,30},{16,0},... | collective-permute-start | bytes 196616 | tf_op jit(solution)/shard_map/ppermute | solution.py:406
  63.2 5.0 %collective-permute-done.2 = f32[128,128]{1,0:T(8,128)S(1)} collective-permute-done((f32[128,128]{1,0:T(8,128)S(1)}, f32[128,128]{1,0:T(8,128)S(1)}, u32[]{:S(2)}, u32[]{:S(2)}) %collective-permute-start.2) | collective-permute-done | bytes 65568 | tf_op jit(solution)/shard_map/ppermute | solution.py:406
  68.2 10.4 %all_to_all.29 = f32[8,128,128]{2,1,0:T(8,128)S(1)} all-to-all(f32[8,128,128]{2,1,0:T(8,128)S(1)} %reshape_tile.3), channel_id=1, replica_groups={{0,2,4,6,8,10,12,14},{16,18,20,22,24,26,28,30},{1,3,5,7,9,11,13,15},{17..., dimensions={0} | all-to-all | bytes 1048576 | tf_op jit(solution)/shard_map/all_to_all | solution.py:369
  78.7 0.3 row_gram.1.mine_ref
  79.0 0.1 collective-permute-start.3
  79.1 0.7 copy.5
  79.7 0.6 collective-permute-done.3.other_ref
  80.3 3.5 %finish.1 = f32[1024,128]{1,0:T(8,128)} custom-call(f32[1024,128]{1,0:T(8,128)S(1)} %bitcast.9, f32[128,128]{1,0:T(8,128)S(1)} %row_gram.1.mine_ref, f32[128,128]{1,0:T(8,128)S(1)} %collective-permute-done.3.other_ref), custom_call_target="tpu_custom_call" | custom-call | tf_op jit(solution)/shard_map/finish/pallas_call | solution.py:338
  (4 shorter events, 0.1 us)
Async XLA Ops:
  3.5 29.4 %copy-start = (f32[16,8]{0,1:T(8,128)S(1)}, f32[16,8]{0,1:T(8,128)}, u32[]{:S(2)}) copy-start(f32[16,8]{0,1:T(8,128)} %param.5) | copy-start | bytes 1540
  3.5 1.7 %collective-permute-start = (f32[16,2,8,256]{3,2,1,0:T(8,128)S(1)}, f32[16,2,8,256]{3,2,1,0:T(8,128)S(1)}, u32[]{:S(2)}, u32[]{:S(2)}) collective-permute-start(f32[16,2,8,256]{3,2,1,0:T(8,128)S(1)} %get-tuple-element.17), channel_id=1, source_target_pairs={{0,1},{1,0},{2,3},{3,2},{4,5},{5,4},{6,7},{7,6},{8,9},{9,8},{10,11... | collective-permute-start | bytes 786440 | tf_op jit(solution)/shard_map/ppermute | solution.py:385
  47.5 1.5 %collective-permute-start.1 = (f32[16,2,8,256]{3,2,1,0:T(8,128)S(1)}, f32[16,2,8,256]{3,2,1,0:T(8,128)S(1)}, u32[]{:S(2)}, u32[]{:S(2)}) collective-permute-start(f32[16,2,8,256]{3,2,1,0:T(8,128)S(1)} %bitcast.13), channel_id=1, source_target_pairs={{0,1},{1,0},{2,3},{3,2},{4,5},{5,4},{6,7},{7,6},{8,9},{9,8},{10,11... | collective-permute-start | bytes 786440 | tf_op jit(solution)/shard_map/ppermute | solution.py:402
  62.2 5.9 %collective-permute-start.2 = (f32[128,128]{1,0:T(8,128)S(1)}, f32[128,128]{1,0:T(8,128)S(1)}, u32[]{:S(2)}, u32[]{:S(2)}) collective-permute-start(f32[128,128]{1,0:T(8,128)S(1)} %reduce_sum.9), channel_id=1, source_target_pairs={{0,16},{2,18},{4,20},{6,22},{8,24},{10,26},{12,28},{14,30},{16,0},... | collective-permute-start | bytes 196616 | tf_op jit(solution)/shard_map/ppermute | solution.py:406
  79.0 1.3 %collective-permute-start.3 = (f32[128,128]{1,0:T(8,128)S(1)}, f32[128,128]{1,0:T(8,128)S(1)}, u32[]{:S(2)}, u32[]{:S(2)}) collective-permute-start(f32[128,128]{1,0:T(8,128)S(1)} %row_gram.1.mine_ref), channel_id=1, source_target_pairs={{0,1},{1,0},{2,3},{3,2},{4,5},{5,4},{6,7},{7,6},{8,9},{9,8},{10,11... | collective-permute-start | bytes 196616 | tf_op jit(solution)/shard_map/ppermute | solution.py:409

commit v7 on v6

--- a/solution.py
+++ b/solution.py
@@ -322,12 +322,16 @@
 
 def finish_kernel(scale, blocks, block_ref, mine_ref, other_ref, out_ref, made_ref, sems):
     rows = block_ref.shape[0] // blocks
-    left = halves_of(block_ref[...])
-    right = stack(orth_factor(mine_ref[...] + other_ref[...]) * scale)
+    high, middle, low = split3(block_ref[...])
+    left, left_more = jnp.concatenate([high, middle], axis=1), jnp.concatenate([high, low], axis=1)
+    high, middle, low = split3(orth_factor(mine_ref[...] + other_ref[...]) * scale)
+    both = jnp.concatenate([high, middle], axis=1)
+    right, right_more = jnp.concatenate([both, both], axis=0), jnp.concatenate([low, high], axis=0)
     copies = []
     for i in range(blocks):
         take = pl.ds(i * rows, rows)
-        made_ref[take] = by_stacked(left[i * rows : (i + 1) * rows], right)
+        part = slice(i * rows, (i + 1) * rows)
+        made_ref[take] = by_stacked(left[part], right) + fastdot(left_more[part], right_more, ((1,), (0,)))
         copies.append(pltpu.make_async_copy(made_ref.at[take], out_ref.at[take], sems.at[i]))
         copies[-1].start()
     for copy in copies:

time: 84.1 us -> 84.2 us (level)
  no operation moved by 1% of the time
where the time goes in v7:
time: 84.2 us; the launch traced here: 83.9 us
  blocking collectives  62.2 us (74%)
  Pallas kernels  11.8 us (14%)
  waiting for transfers between devices  6.84 us (8%)
  starting transfers between devices  1.58 us (2%)
    all_to_all x2, blocking collectives, to_owners(): lax.all_to_all(flat, ('grp', 'rep'), split_axis=0, concat_axis=0, tiled=T...  29.9 us
    all_to_all x2, blocking collectives, all_to_all(): lax.all_to_all(value, 'grp', split_axis=0, concat_axis=0, tiled=True, axi...  22.9 us
    all_to_all x1, blocking collectives, on_device(): lax.all_to_all(small_gram(owned, groups_n, (devices, 1, groups_n * groups...  9.46 us
    ppermute x1, waiting for transfers between devices, on_device(): chunk = chunk + lax.ppermute(chunk, 'grp', across)  4.98 us
    pallas_call x1, Pallas kernels, finish(): pl.pallas_call(functools.partial(finish_kernel, scale, blocks), out_shape...  3.59 us
    pallas_call x1, Pallas kernels, project_first(): pl.pallas_call(first_kernel, in_specs=[pl.BlockSpec(memory_space=pl.ANY),...  2.83 us
    pallas_call x1, Pallas kernels, mix(): pl.pallas_call(functools.partial(mix_kernel, groups_n), out_shape=(jax.Sh...  2.42 us
  transfers between devices with their start and end apart: 4, of which 4 were waited for; matrix products, arithmetic and copies ran while one was open for 1% of the time, Pallas kernels for 2%

profile of v7, /device:TPU:0, one launch (start us, length us, event | category | flops | bytes accessed | tf_op | source)
XLA Modules:
  0.0 83.9 jit_solution(2456874639451551769)
XLA Ops:
  0.6 2.8 %project_first.1 = (f32[16,2,8,256]{3,2,1,0:T(8,128)S(1)}, bf16[1024,512]{1,0:T(8,128)(2,1)S(1)}, bf16[1024,512]{1,0:T(8,128)(2,1)S(1)}, f32[1024,1024]{1,0:T(8,128)S(1)}, bf16[1024,256]{1,0:T(8,128)(2,1)S(1)}) custom-call(f32[1024,1024]{1,0:T(8,128)} %bitcast.17, f32[1024,128]{1,0:T(8,128)} %factor_ref.1), custom_call_target="tpu_custom_call" | custom-call | tf_op jit(solution)/shard_map/project_first/pallas_call | solution.py:156
  3.5 0.0 copy-start
  3.5 0.6 collective-permute-start
  4.0 0.7 project_second.1
  4.7 0.5 collective-permute-done
  5.2 17.6 %all_to_all.25 = f32[32,8,256]{2,1,0:T(8,128)S(1)} all-to-all(f32[32,8,256]{2,1,0:T(8,128)S(1)} %bitcast.18), channel_id=1, replica_groups=mesh['grp'=16,'rep'=2] {'grp','rep'}, dimensions={0} | all-to-all | bytes 524288 | tf_op jit(solution)/shard_map/all_to_all | solution.py:380
  22.8 0.5 small_gram.1
  23.4 9.5 %all_to_all.26.gram_ref = f32[32,1,256]{2,1,0:T(1,128)S(1)} all-to-all(f32[32,1,256]{2,1,0:T(1,128)S(1)} %small_gram.1), channel_id=1, replica_groups=mesh['grp'=16,'rep'=2] {'grp','rep'}, dimensions={0} | all-to-all | bytes 65536 | tf_op jit(solution)/shard_map/all_to_all | solution.py:395
  32.8 0.0 copy-done
  32.8 2.4 %mix.1 = (f32[16,2,8,256]{3,2,1,0:T(8,128)S(1)}, f32[16,8]{1,0:T(8,128)S(1)}) custom-call(f32[32,1,256]{2,1,0:T(1,128)S(1)} %all_to_all.26.gram_ref, f32[8,16]{1,0:T(8,128)S(1)} %bitcast.16, f32[16,2,8,256]{3,2,1,0:T(8,128)S(1)} %bitcast.11), custom_call_target="tpu_custom_call" | custom-call | tf_op jit(solution)/shard_map/mix/pallas_call | solution.py:315
  35.3 12.3 %all_to_all.27 = f32[32,8,256]{2,1,0:T(8,128)S(1)} all-to-all(f32[32,8,256]{2,1,0:T(8,128)S(1)} %bitcast.15), channel_id=1, replica_groups=mesh['grp'=16,'rep'=2] {'grp','rep'}, dimensions={0} | all-to-all | bytes 524288 | tf_op jit(solution)/shard_map/all_to_all | solution.py:380
  47.5 0.0 collective-permute-start.1
  47.5 0.7 multiply.2.refs_0_
  48.3 0.8 collective-permute-done.1.weight_ref
  49.1 0.7 multiply.3
  49.8 12.4 %all_to_all.28 = f32[8,128,128]{2,1,0:T(8,128)S(1)} all-to-all(f32[8,128,128]{2,1,0:T(8,128)S(1)} %bitcast.12), channel_id=1, replica_groups={{0,2,4,6,8,10,12,14},{16,18,20,22,24,26,28,30},{1,3,5,7,9,11,13,15},{17..., dimensions={0} | all-to-all | bytes 1048576 | tf_op jit(solution)/shard_map/all_to_all | solution.py:373
  62.2 0.9 %collective-permute-start.2 = (f32[128,128]{1,0:T(8,128)S(1)}, f32[128,128]{1,0:T(8,128)S(1)}, u32[]{:S(2)}, u32[]{:S(2)}) collective-permute-start(f32[128,128]{1,0:T(8,128)S(1)} %reduce_sum.9), channel_id=1, source_target_pairs={{0,16},{2,18},{4,20},{6,22},{8,24},{10,26},{12,28},{14,30},{16,0},... | collective-permute-start | bytes 196616 | tf_op jit(solution)/shard_map/ppermute | solution.py:410
  63.2 5.0 %collective-permute-done.2 = f32[128,128]{1,0:T(8,128)S(1)} collective-permute-done((f32[128,128]{1,0:T(8,128)S(1)}, f32[128,128]{1,0:T(8,128)S(1)}, u32[]{:S(2)}, u32[]{:S(2)}) %collective-permute-start.2) | collective-permute-done | bytes 65568 | tf_op jit(solution)/shard_map/ppermute | solution.py:410
  68.2 10.4 %all_to_all.29 = f32[8,128,128]{2,1,0:T(8,128)S(1)} all-to-all(f32[8,128,128]{2,1,0:T(8,128)S(1)} %reshape_tile.3), channel_id=1, replica_groups={{0,2,4,6,8,10,12,14},{16,18,20,22,24,26,28,30},{1,3,5,7,9,11,13,15},{17..., dimensions={0} | all-to-all | bytes 1048576 | tf_op jit(solution)/shard_map/all_to_all | solution.py:373
  78.7 0.3 row_gram.1.mine_ref
  79.0 0.1 collective-permute-start.3
  79.1 0.7 copy.5
  79.7 0.6 collective-permute-done.3.other_ref
  80.3 3.6 %finish.1 = f32[1024,128]{1,0:T(8,128)} custom-call(f32[1024,128]{1,0:T(8,128)S(1)} %bitcast.9, f32[128,128]{1,0:T(8,128)S(1)} %row_gram.1.mine_ref, f32[128,128]{1,0:T(8,128)S(1)} %collective-permute-done.3.other_ref), custom_call_target="tpu_custom_call" | custom-call | tf_op jit(solution)/shard_map/finish/pallas_call | solution.py:342
  (4 shorter events, 0.1 us)
Async XLA Ops:
  3.5 29.4 %copy-start = (f32[16,8]{0,1:T(8,128)S(1)}, f32[16,8]{0,1:T(8,128)}, u32[]{:S(2)}) copy-start(f32[16,8]{0,1:T(8,128)} %param.5) | copy-start | bytes 1540
  3.5 1.7 %collective-permute-start = (f32[16,2,8,256]{3,2,1,0:T(8,128)S(1)}, f32[16,2,8,256]{3,2,1,0:T(8,128)S(1)}, u32[]{:S(2)}, u32[]{:S(2)}) collective-permute-start(f32[16,2,8,256]{3,2,1,0:T(8,128)S(1)} %get-tuple-element.17), channel_id=1, source_target_pairs={{0,1},{1,0},{2,3},{3,2},{4,5},{5,4},{6,7},{7,6},{8,9},{9,8},{10,11... | collective-permute-start | bytes 786440 | tf_op jit(solution)/shard_map/ppermute | solution.py:389
  47.5 1.5 %collective-permute-start.1 = (f32[16,2,8,256]{3,2,1,0:T(8,128)S(1)}, f32[16,2,8,256]{3,2,1,0:T(8,128)S(1)}, u32[]{:S(2)}, u32[]{:S(2)}) collective-permute-start(f32[16,2,8,256]{3,2,1,0:T(8,128)S(1)} %bitcast.13), channel_id=1, source_target_pairs={{0,1},{1,0},{2,3},{3,2},{4,5},{5,4},{6,7},{7,6},{8,9},{9,8},{10,11... | collective-permute-start | bytes 786440 | tf_op jit(solution)/shard_map/ppermute | solution.py:406
  62.2 5.9 %collective-permute-start.2 = (f32[128,128]{1,0:T(8,128)S(1)}, f32[128,128]{1,0:T(8,128)S(1)}, u32[]{:S(2)}, u32[]{:S(2)}) collective-permute-start(f32[128,128]{1,0:T(8,128)S(1)} %reduce_sum.9), channel_id=1, source_target_pairs={{0,16},{2,18},{4,20},{6,22},{8,24},{10,26},{12,28},{14,30},{16,0},... | collective-permute-start | bytes 196616 | tf_op jit(solution)/shard_map/ppermute | solution.py:410
  79.0 1.3 %collective-permute-start.3 = (f32[128,128]{1,0:T(8,128)S(1)}, f32[128,128]{1,0:T(8,128)S(1)}, u32[]{:S(2)}, u32[]{:S(2)}) collective-permute-start(f32[128,128]{1,0:T(8,128)S(1)} %row_gram.1.mine_ref), channel_id=1, source_target_pairs={{0,1},{1,0},{2,3},{3,2},{4,5},{5,4},{6,7},{7,6},{8,9},{9,8},{10,11... | collective-permute-start | bytes 196616 | tf_op jit(solution)/shard_map/ppermute | solution.py:413

commit v8 on v7

--- a/solution.py
+++ b/solution.py
@@ -298,7 +298,12 @@
         columns = dot(time_ref[...], cells(groups_n, count, lambda row: row, lambda cell: cell % groups_n))
         start = dot(rows, columns, ((1,), (1,)))
         turned = dot(columns, rows, ((1,), (1,)))
-    basis = dot(start, orth_factor(dot(turned, start) * (1.0 / per)))
+    factor = orth_factor(dot(turned, start) * (1.0 / per))
+    size = factor.shape[0]
+    if size <= 16:
+        basis = tree_sum([start[:, k : k + 1] * factor[k : k + 1] for k in range(size)])
+    else:
+        basis = dot(start, factor)
     mixer = jnp.where(same_slot(groups_n, rank), dot(basis, basis, ((1,), (1,))), 0.0)
     mixer_high, mixer_low = split(mixer)
     mixed = fastdot(

time: 84.2 us -> 83.9 us (level)
  no operation moved by 1% of the time
where the time goes in v8:
time: 83.9 us; the launch traced here: 83.7 us
  blocking collectives  62.2 us (74%)
  Pallas kernels  11.6 us (14%)
  waiting for transfers between devices  6.84 us (8%)
  starting transfers between devices  1.58 us (2%)
    all_to_all x2, blocking collectives, to_owners(): lax.all_to_all(flat, ('grp', 'rep'), split_axis=0, concat_axis=0, tiled=T...  29.9 us
    all_to_all x2, blocking collectives, all_to_all(): lax.all_to_all(value, 'grp', split_axis=0, concat_axis=0, tiled=True, axi...  22.9 us
    all_to_all x1, blocking collectives, on_device(): lax.all_to_all(small_gram(owned, groups_n, (devices, 1, groups_n * groups...  9.46 us
    ppermute x1, waiting for transfers between devices, on_device(): chunk = chunk + lax.ppermute(chunk, 'grp', across)  4.98 us
    pallas_call x1, Pallas kernels, finish(): pl.pallas_call(functools.partial(finish_kernel, scale, blocks), out_shape...  3.59 us
    pallas_call x1, Pallas kernels, project_first(): pl.pallas_call(first_kernel, in_specs=[pl.BlockSpec(memory_space=pl.ANY),...  2.83 us
    pallas_call x1, Pallas kernels, mix(): pl.pallas_call(functools.partial(mix_kernel, groups_n), out_shape=(jax.Sh...  2.21 us
  transfers between devices with their start and end apart: 4, of which 4 were waited for; matrix products, arithmetic and copies ran while one was open for 1% of the time, Pallas kernels for 2%

profile of v8, /device:TPU:0, one launch (start us, length us, event | category | flops | bytes accessed | tf_op | source)
XLA Modules:
  0.0 83.7 jit_solution(17749617944159848328)
XLA Ops:
  0.6 2.8 %project_first.1 = (f32[16,2,8,256]{3,2,1,0:T(8,128)S(1)}, bf16[1024,512]{1,0:T(8,128)(2,1)S(1)}, bf16[1024,512]{1,0:T(8,128)(2,1)S(1)}, f32[1024,1024]{1,0:T(8,128)S(1)}, bf16[1024,256]{1,0:T(8,128)(2,1)S(1)}) custom-call(f32[1024,1024]{1,0:T(8,128)} %bitcast.17, f32[1024,128]{1,0:T(8,128)} %factor_ref.1), custom_call_target="tpu_custom_call" | custom-call | tf_op jit(solution)/shard_map/project_first/pallas_call | solution.py:156
  3.5 0.0 copy-start
  3.5 0.6 collective-permute-start
  4.0 0.7 project_second.1
  4.7 0.5 collective-permute-done
  5.2 17.6 %all_to_all.25 = f32[32,8,256]{2,1,0:T(8,128)S(1)} all-to-all(f32[32,8,256]{2,1,0:T(8,128)S(1)} %bitcast.18), channel_id=1, replica_groups=mesh['grp'=16,'rep'=2] {'grp','rep'}, dimensions={0} | all-to-all | bytes 524288 | tf_op jit(solution)/shard_map/all_to_all | solution.py:385
  22.8 0.5 small_gram.1
  23.4 9.5 %all_to_all.26.gram_ref = f32[32,1,256]{2,1,0:T(1,128)S(1)} all-to-all(f32[32,1,256]{2,1,0:T(1,128)S(1)} %small_gram.1), channel_id=1, replica_groups=mesh['grp'=16,'rep'=2] {'grp','rep'}, dimensions={0} | all-to-all | bytes 65536 | tf_op jit(solution)/shard_map/all_to_all | solution.py:400
  32.8 0.0 copy-done
  32.8 2.2 %mix.1 = (f32[16,2,8,256]{3,2,1,0:T(8,128)S(1)}, f32[16,8]{1,0:T(8,128)S(1)}) custom-call(f32[32,1,256]{2,1,0:T(1,128)S(1)} %all_to_all.26.gram_ref, f32[8,16]{1,0:T(8,128)S(1)} %bitcast.16, f32[16,2,8,256]{3,2,1,0:T(8,128)S(1)} %bitcast.11), custom_call_target="tpu_custom_call" | custom-call | tf_op jit(solution)/shard_map/mix/pallas_call | solution.py:320
  35.0 12.3 %all_to_all.27 = f32[32,8,256]{2,1,0:T(8,128)S(1)} all-to-all(f32[32,8,256]{2,1,0:T(8,128)S(1)} %bitcast.15), channel_id=1, replica_groups=mesh['grp'=16,'rep'=2] {'grp','rep'}, dimensions={0} | all-to-all | bytes 524288 | tf_op jit(solution)/shard_map/all_to_all | solution.py:385
  47.3 0.0 collective-permute-start.1
  47.3 0.7 multiply.2.refs_0_
  48.0 0.8 collective-permute-done.1.weight_ref
  48.8 0.7 multiply.3
  49.6 12.4 %all_to_all.28 = f32[8,128,128]{2,1,0:T(8,128)S(1)} all-to-all(f32[8,128,128]{2,1,0:T(8,128)S(1)} %bitcast.12), channel_id=1, replica_groups={{0,2,4,6,8,10,12,14},{16,18,20,22,24,26,28,30},{1,3,5,7,9,11,13,15},{17..., dimensions={0} | all-to-all | bytes 1048576 | tf_op jit(solution)/shard_map/all_to_all | solution.py:378
  62.0 0.9 %collective-permute-start.2 = (f32[128,128]{1,0:T(8,128)S(1)}, f32[128,128]{1,0:T(8,128)S(1)}, u32[]{:S(2)}, u32[]{:S(2)}) collective-permute-start(f32[128,128]{1,0:T(8,128)S(1)} %reduce_sum.9), channel_id=1, source_target_pairs={{0,16},{2,18},{4,20},{6,22},{8,24},{10,26},{12,28},{14,30},{16,0},... | collective-permute-start | bytes 196616 | tf_op jit(solution)/shard_map/ppermute | solution.py:415
  63.0 5.0 %collective-permute-done.2 = f32[128,128]{1,0:T(8,128)S(1)} collective-permute-done((f32[128,128]{1,0:T(8,128)S(1)}, f32[128,128]{1,0:T(8,128)S(1)}, u32[]{:S(2)}, u32[]{:S(2)}) %collective-permute-start.2) | collective-permute-done | bytes 65568 | tf_op jit(solution)/shard_map/ppermute | solution.py:415
  68.0 10.4 %all_to_all.29 = f32[8,128,128]{2,1,0:T(8,128)S(1)} all-to-all(f32[8,128,128]{2,1,0:T(8,128)S(1)} %reshape_tile.3), channel_id=1, replica_groups={{0,2,4,6,8,10,12,14},{16,18,20,22,24,26,28,30},{1,3,5,7,9,11,13,15},{17..., dimensions={0} | all-to-all | bytes 1048576 | tf_op jit(solution)/shard_map/all_to_all | solution.py:378
  78.4 0.3 row_gram.1.mine_ref
  78.8 0.1 collective-permute-start.3
  78.9 0.7 copy.5
  79.5 0.6 collective-permute-done.3.other_ref
  80.1 3.6 %finish.1 = f32[1024,128]{1,0:T(8,128)} custom-call(f32[1024,128]{1,0:T(8,128)S(1)} %bitcast.9, f32[128,128]{1,0:T(8,128)S(1)} %row_gram.1.mine_ref, f32[128,128]{1,0:T(8,128)S(1)} %collective-permute-done.3.other_ref), custom_call_target="tpu_custom_call" | custom-call | tf_op jit(solution)/shard_map/finish/pallas_call | solution.py:347
  (4 shorter events, 0.1 us)
Async XLA Ops:
  3.5 29.4 %copy-start = (f32[16,8]{0,1:T(8,128)S(1)}, f32[16,8]{0,1:T(8,128)}, u32[]{:S(2)}) copy-start(f32[16,8]{0,1:T(8,128)} %param.5) | copy-start | bytes 1540
  3.5 1.7 %collective-permute-start = (f32[16,2,8,256]{3,2,1,0:T(8,128)S(1)}, f32[16,2,8,256]{3,2,1,0:T(8,128)S(1)}, u32[]{:S(2)}, u32[]{:S(2)}) collective-permute-start(f32[16,2,8,256]{3,2,1,0:T(8,128)S(1)} %get-tuple-element.17), channel_id=1, source_target_pairs={{0,1},{1,0},{2,3},{3,2},{4,5},{5,4},{6,7},{7,6},{8,9},{9,8},{10,11... | collective-permute-start | bytes 786440 | tf_op jit(solution)/shard_map/ppermute | solution.py:394
  47.3 1.5 %collective-permute-start.1 = (f32[16,2,8,256]{3,2,1,0:T(8,128)S(1)}, f32[16,2,8,256]{3,2,1,0:T(8,128)S(1)}, u32[]{:S(2)}, u32[]{:S(2)}) collective-permute-start(f32[16,2,8,256]{3,2,1,0:T(8,128)S(1)} %bitcast.13), channel_id=1, source_target_pairs={{0,1},{1,0},{2,3},{3,2},{4,5},{5,4},{6,7},{7,6},{8,9},{9,8},{10,11... | collective-permute-start | bytes 786440 | tf_op jit(solution)/shard_map/ppermute | solution.py:411
  62.0 5.9 %collective-permute-start.2 = (f32[128,128]{1,0:T(8,128)S(1)}, f32[128,128]{1,0:T(8,128)S(1)}, u32[]{:S(2)}, u32[]{:S(2)}) collective-permute-start(f32[128,128]{1,0:T(8,128)S(1)} %reduce_sum.9), channel_id=1, source_target_pairs={{0,16},{2,18},{4,20},{6,22},{8,24},{10,26},{12,28},{14,30},{16,0},... | collective-permute-start | bytes 196616 | tf_op jit(solution)/shard_map/ppermute | solution.py:415
  78.8 1.3 %collective-permute-start.3 = (f32[128,128]{1,0:T(8,128)S(1)}, f32[128,128]{1,0:T(8,128)S(1)}, u32[]{:S(2)}, u32[]{:S(2)}) collective-permute-start(f32[128,128]{1,0:T(8,128)S(1)} %row_gram.1.mine_ref), channel_id=1, source_target_pairs={{0,1},{1,0},{2,3},{3,2},{4,5},{5,4},{6,7},{7,6},{8,9},{9,8},{10,11... | collective-permute-start | bytes 196616 | tf_op jit(solution)/shard_map/ppermute | solution.py:418

commit v9 on v8

--- a/solution.py
+++ b/solution.py
@@ -302,9 +302,12 @@
     size = factor.shape[0]
     if size <= 16:
         basis = tree_sum([start[:, k : k + 1] * factor[k : k + 1] for k in range(size)])
+        basis_turned = tree_sum([factor[:, k : k + 1] * turned[k : k + 1] for k in range(size)])
+        outer = tree_sum([basis[:, k : k + 1] * basis_turned[k : k + 1] for k in range(size)])
     else:
         basis = dot(start, factor)
-    mixer = jnp.where(same_slot(groups_n, rank), dot(basis, basis, ((1,), (1,))), 0.0)
+        outer = dot(basis, basis, ((1,), (1,)))
+    mixer = jnp.where(same_slot(groups_n, rank), outer, 0.0)
     mixer_high, mixer_low = split(mixer)
     mixed = fastdot(
         jnp.concatenate([mixer_high, mixer_low, mixer_high], axis=1),

time: 83.9 us -> 83.8 us (level)
  no operation moved by 1% of the time
where the time goes in v9:
time: 83.8 us; the launch traced here: 83.6 us
  blocking collectives  62.2 us (74%)
  Pallas kernels  11.5 us (14%)
  waiting for transfers between devices  6.84 us (8%)
  starting transfers between devices  1.58 us (2%)
    all_to_all x2, blocking collectives, to_owners(): lax.all_to_all(flat, ('grp', 'rep'), split_axis=0, concat_axis=0, tiled=T...  29.9 us
    all_to_all x2, blocking collectives, all_to_all(): lax.all_to_all(value, 'grp', split_axis=0, concat_axis=0, tiled=True, axi...  22.9 us
    all_to_all x1, blocking collectives, on_device(): lax.all_to_all(small_gram(owned, groups_n, (devices, 1, groups_n * groups...  9.46 us
    ppermute x1, waiting for transfers between devices, on_device(): chunk = chunk + lax.ppermute(chunk, 'grp', across)  4.98 us
    pallas_call x1, Pallas kernels, finish(): pl.pallas_call(functools.partial(finish_kernel, scale, blocks), out_shape...  3.59 us
    pallas_call x1, Pallas kernels, project_first(): pl.pallas_call(first_kernel, in_specs=[pl.BlockSpec(memory_space=pl.ANY),...  2.83 us
    pallas_call x1, Pallas kernels, mix(): pl.pallas_call(functools.partial(mix_kernel, groups_n), out_shape=(jax.Sh...  2.08 us
  transfers between devices with their start and end apart: 4, of which 4 were waited for; matrix products, arithmetic and copies ran while one was open for 1% of the time, Pallas kernels for 2%

profile of v9, /device:TPU:0, one launch (start us, length us, event | category | flops | bytes accessed | tf_op | source)
XLA Modules:
  0.0 83.6 jit_solution(6507067848908274879)
XLA Ops:
  0.6 2.8 %project_first.1 = (f32[16,2,8,256]{3,2,1,0:T(8,128)S(1)}, bf16[1024,512]{1,0:T(8,128)(2,1)S(1)}, bf16[1024,512]{1,0:T(8,128)(2,1)S(1)}, f32[1024,1024]{1,0:T(8,128)S(1)}, bf16[1024,256]{1,0:T(8,128)(2,1)S(1)}) custom-call(f32[1024,1024]{1,0:T(8,128)} %bitcast.17, f32[1024,128]{1,0:T(8,128)} %factor_ref.1), custom_call_target="tpu_custom_call" | custom-call | tf_op jit(solution)/shard_map/project_first/pallas_call | solution.py:156
  3.5 0.0 copy-start
  3.5 0.6 collective-permute-start
  4.0 0.7 project_second.1
  4.7 0.5 collective-permute-done
  5.2 17.6 %all_to_all.25 = f32[32,8,256]{2,1,0:T(8,128)S(1)} all-to-all(f32[32,8,256]{2,1,0:T(8,128)S(1)} %bitcast.18), channel_id=1, replica_groups=mesh['grp'=16,'rep'=2] {'grp','rep'}, dimensions={0} | all-to-all | bytes 524288 | tf_op jit(solution)/shard_map/all_to_all | solution.py:388
  22.8 0.5 small_gram.1
  23.4 9.5 %all_to_all.26.gram_ref = f32[32,1,256]{2,1,0:T(1,128)S(1)} all-to-all(f32[32,1,256]{2,1,0:T(1,128)S(1)} %small_gram.1), channel_id=1, replica_groups=mesh['grp'=16,'rep'=2] {'grp','rep'}, dimensions={0} | all-to-all | bytes 65536 | tf_op jit(solution)/shard_map/all_to_all | solution.py:403
  32.8 0.0 copy-done
  32.8 2.1 %mix.1 = (f32[16,2,8,256]{3,2,1,0:T(8,128)S(1)}, f32[16,8]{1,0:T(8,128)S(1)}) custom-call(f32[32,1,256]{2,1,0:T(1,128)S(1)} %all_to_all.26.gram_ref, f32[8,16]{1,0:T(8,128)S(1)} %bitcast.16, f32[16,2,8,256]{3,2,1,0:T(8,128)S(1)} %bitcast.11), custom_call_target="tpu_custom_call" | custom-call | tf_op jit(solution)/shard_map/mix/pallas_call | solution.py:323
  34.9 12.3 %all_to_all.27 = f32[32,8,256]{2,1,0:T(8,128)S(1)} all-to-all(f32[32,8,256]{2,1,0:T(8,128)S(1)} %bitcast.15), channel_id=1, replica_groups=mesh['grp'=16,'rep'=2] {'grp','rep'}, dimensions={0} | all-to-all | bytes 524288 | tf_op jit(solution)/shard_map/all_to_all | solution.py:388
  47.2 0.0 collective-permute-start.1
  47.2 0.7 multiply.2.refs_0_
  47.9 0.8 collective-permute-done.1.weight_ref
  48.7 0.7 multiply.3
  49.5 12.4 %all_to_all.28 = f32[8,128,128]{2,1,0:T(8,128)S(1)} all-to-all(f32[8,128,128]{2,1,0:T(8,128)S(1)} %bitcast.12), channel_id=1, replica_groups={{0,2,4,6,8,10,12,14},{16,18,20,22,24,26,28,30},{1,3,5,7,9,11,13,15},{17..., dimensions={0} | all-to-all | bytes 1048576 | tf_op jit(solution)/shard_map/all_to_all | solution.py:381
  61.9 0.9 %collective-permute-start.2 = (f32[128,128]{1,0:T(8,128)S(1)}, f32[128,128]{1,0:T(8,128)S(1)}, u32[]{:S(2)}, u32[]{:S(2)}) collective-permute-start(f32[128,128]{1,0:T(8,128)S(1)} %reduce_sum.9), channel_id=1, source_target_pairs={{0,16},{2,18},{4,20},{6,22},{8,24},{10,26},{12,28},{14,30},{16,0},... | collective-permute-start | bytes 196616 | tf_op jit(solution)/shard_map/ppermute | solution.py:418
  62.9 5.0 %collective-permute-done.2 = f32[128,128]{1,0:T(8,128)S(1)} collective-permute-done((f32[128,128]{1,0:T(8,128)S(1)}, f32[128,128]{1,0:T(8,128)S(1)}, u32[]{:S(2)}, u32[]{:S(2)}) %collective-permute-start.2) | collective-permute-done | bytes 65568 | tf_op jit(solution)/shard_map/ppermute | solution.py:418
  67.9 10.4 %all_to_all.29 = f32[8,128,128]{2,1,0:T(8,128)S(1)} all-to-all(f32[8,128,128]{2,1,0:T(8,128)S(1)} %reshape_tile.3), channel_id=1, replica_groups={{0,2,4,6,8,10,12,14},{16,18,20,22,24,26,28,30},{1,3,5,7,9,11,13,15},{17..., dimensions={0} | all-to-all | bytes 1048576 | tf_op jit(solution)/shard_map/all_to_all | solution.py:381
  78.3 0.3 row_gram.1.mine_ref
  78.7 0.1 collective-permute-start.3
  78.8 0.7 copy.5
  79.4 0.6 collective-permute-done.3.other_ref
  80.0 3.6 %finish.1 = f32[1024,128]{1,0:T(8,128)} custom-call(f32[1024,128]{1,0:T(8,128)S(1)} %bitcast.9, f32[128,128]{1,0:T(8,128)S(1)} %row_gram.1.mine_ref, f32[128,128]{1,0:T(8,128)S(1)} %collective-permute-done.3.other_ref), custom_call_target="tpu_custom_call" | custom-call | tf_op jit(solution)/shard_map/finish/pallas_call | solution.py:350
  (4 shorter events, 0.1 us)
Async XLA Ops:
  3.5 29.4 %copy-start = (f32[16,8]{0,1:T(8,128)S(1)}, f32[16,8]{0,1:T(8,128)}, u32[]{:S(2)}) copy-start(f32[16,8]{0,1:T(8,128)} %param.5) | copy-start | bytes 1540
  3.5 1.7 %collective-permute-start = (f32[16,2,8,256]{3,2,1,0:T(8,128)S(1)}, f32[16,2,8,256]{3,2,1,0:T(8,128)S(1)}, u32[]{:S(2)}, u32[]{:S(2)}) collective-permute-start(f32[16,2,8,256]{3,2,1,0:T(8,128)S(1)} %get-tuple-element.17), channel_id=1, source_target_pairs={{0,1},{1,0},{2,3},{3,2},{4,5},{5,4},{6,7},{7,6},{8,9},{9,8},{10,11... | collective-permute-start | bytes 786440 | tf_op jit(solution)/shard_map/ppermute | solution.py:397
  47.2 1.5 %collective-permute-start.1 = (f32[16,2,8,256]{3,2,1,0:T(8,128)S(1)}, f32[16,2,8,256]{3,2,1,0:T(8,128)S(1)}, u32[]{:S(2)}, u32[]{:S(2)}) collective-permute-start(f32[16,2,8,256]{3,2,1,0:T(8,128)S(1)} %bitcast.13), channel_id=1, source_target_pairs={{0,1},{1,0},{2,3},{3,2},{4,5},{5,4},{6,7},{7,6},{8,9},{9,8},{10,11... | collective-permute-start | bytes 786440 | tf_op jit(solution)/shard_map/ppermute | solution.py:414
  61.9 5.9 %collective-permute-start.2 = (f32[128,128]{1,0:T(8,128)S(1)}, f32[128,128]{1,0:T(8,128)S(1)}, u32[]{:S(2)}, u32[]{:S(2)}) collective-permute-start(f32[128,128]{1,0:T(8,128)S(1)} %reduce_sum.9), channel_id=1, source_target_pairs={{0,16},{2,18},{4,20},{6,22},{8,24},{10,26},{12,28},{14,30},{16,0},... | collective-permute-start | bytes 196616 | tf_op jit(solution)/shard_map/ppermute | solution.py:418
  78.7 1.3 %collective-permute-start.3 = (f32[128,128]{1,0:T(8,128)S(1)}, f32[128,128]{1,0:T(8,128)S(1)}, u32[]{:S(2)}, u32[]{:S(2)}) collective-permute-start(f32[128,128]{1,0:T(8,128)S(1)} %row_gram.1.mine_ref), channel_id=1, source_target_pairs={{0,1},{1,0},{2,3},{3,2},{4,5},{5,4},{6,7},{7,6},{8,9},{9,8},{10,11... | collective-permute-start | bytes 196616 | tf_op jit(solution)/shard_map/ppermute | solution.py:421

commit v10 on v9

--- a/solution.py
+++ b/solution.py
@@ -66,9 +66,9 @@
 def small_step(squared, factor, unit):
     size = unit.shape[0]
     columns = [jnp.broadcast_to(squared[:, k : k + 1], unit.shape) for k in range(size)]
-    turn = 1.5 * unit - 0.5 * squared
     turn_columns = [1.5 * unit[:, k : k + 1] - 0.5 * columns[k] for k in range(size)]
-    turn_squared = tree_sum([turn_columns[k] * turn[k : k + 1] for k in range(size)])
+    turn_rows = [1.5 * unit[k : k + 1] - 0.5 * jnp.broadcast_to(squared[k : k + 1], unit.shape) for k in range(size)]
+    turn_squared = tree_sum([turn_columns[k] * turn_rows[k] for k in range(size)])
     factor = tree_sum([turn_columns[k] * factor[k : k + 1] for k in range(size)])
     return tree_sum([columns[k] * turn_squared[k : k + 1] for k in range(size)]), factor
 

time: 83.8 us -> 83.8 us (level)
  no operation moved by 1% of the time
where the time goes in v10:
time: 83.8 us; the launch traced here: 83.6 us
  blocking collectives  62.2 us (74%)
  Pallas kernels  11.5 us (14%)
  waiting for transfers between devices  6.84 us (8%)
  starting transfers between devices  1.58 us (2%)
    all_to_all x2, blocking collectives, to_owners(): lax.all_to_all(flat, ('grp', 'rep'), split_axis=0, concat_axis=0, tiled=T...  29.9 us
    all_to_all x2, blocking collectives, all_to_all(): lax.all_to_all(value, 'grp', split_axis=0, concat_axis=0, tiled=True, axi...  22.9 us
    all_to_all x1, blocking collectives, on_device(): lax.all_to_all(small_gram(owned, groups_n, (devices, 1, groups_n * groups...  9.46 us
    ppermute x1, waiting for transfers between devices, on_device(): chunk = chunk + lax.ppermute(chunk, 'grp', across)  4.98 us
    pallas_call x1, Pallas kernels, finish(): pl.pallas_call(functools.partial(finish_kernel, scale, blocks), out_shape...  3.59 us
    pallas_call x1, Pallas kernels, project_first(): pl.pallas_call(first_kernel, in_specs=[pl.BlockSpec(memory_space=pl.ANY),...  2.83 us
    pallas_call x1, Pallas kernels, mix(): pl.pallas_call(functools.partial(mix_kernel, groups_n), out_shape=(jax.Sh...  2.08 us
  transfers between devices with their start and end apart: 4, of which 4 were waited for; matrix products, arithmetic and copies ran while one was open for 1% of the time, Pallas kernels for 2%

profile of v10, /device:TPU:0, one launch (start us, length us, event | category | flops | bytes accessed | tf_op | source)
XLA Modules:
  0.0 83.6 jit_solution(12899326469109146937)
XLA Ops:
  0.6 2.8 %project_first.1 = (f32[16,2,8,256]{3,2,1,0:T(8,128)S(1)}, bf16[1024,512]{1,0:T(8,128)(2,1)S(1)}, bf16[1024,512]{1,0:T(8,128)(2,1)S(1)}, f32[1024,1024]{1,0:T(8,128)S(1)}, bf16[1024,256]{1,0:T(8,128)(2,1)S(1)}) custom-call(f32[1024,1024]{1,0:T(8,128)} %bitcast.17, f32[1024,128]{1,0:T(8,128)} %factor_ref.1), custom_call_target="tpu_custom_call" | custom-call | tf_op jit(solution)/shard_map/project_first/pallas_call | solution.py:156
  3.5 0.0 copy-start
  3.5 0.6 collective-permute-start
  4.0 0.7 project_second.1
  4.7 0.5 collective-permute-done
  5.2 17.6 %all_to_all.25 = f32[32,8,256]{2,1,0:T(8,128)S(1)} all-to-all(f32[32,8,256]{2,1,0:T(8,128)S(1)} %bitcast.18), channel_id=1, replica_groups=mesh['grp'=16,'rep'=2] {'grp','rep'}, dimensions={0} | all-to-all | bytes 524288 | tf_op jit(solution)/shard_map/all_to_all | solution.py:388
  22.8 0.5 small_gram.1
  23.4 9.5 %all_to_all.26.gram_ref = f32[32,1,256]{2,1,0:T(1,128)S(1)} all-to-all(f32[32,1,256]{2,1,0:T(1,128)S(1)} %small_gram.1), channel_id=1, replica_groups=mesh['grp'=16,'rep'=2] {'grp','rep'}, dimensions={0} | all-to-all | bytes 65536 | tf_op jit(solution)/shard_map/all_to_all | solution.py:403
  32.8 0.0 copy-done
  32.8 2.1 %mix.1 = (f32[16,2,8,256]{3,2,1,0:T(8,128)S(1)}, f32[16,8]{1,0:T(8,128)S(1)}) custom-call(f32[32,1,256]{2,1,0:T(1,128)S(1)} %all_to_all.26.gram_ref, f32[8,16]{1,0:T(8,128)S(1)} %bitcast.16, f32[16,2,8,256]{3,2,1,0:T(8,128)S(1)} %bitcast.11), custom_call_target="tpu_custom_call" | custom-call | tf_op jit(solution)/shard_map/mix/pallas_call | solution.py:323
  34.9 12.3 %all_to_all.27 = f32[32,8,256]{2,1,0:T(8,128)S(1)} all-to-all(f32[32,8,256]{2,1,0:T(8,128)S(1)} %bitcast.15), channel_id=1, replica_groups=mesh['grp'=16,'rep'=2] {'grp','rep'}, dimensions={0} | all-to-all | bytes 524288 | tf_op jit(solution)/shard_map/all_to_all | solution.py:388
  47.2 0.0 collective-permute-start.1
  47.2 0.7 multiply.2.refs_0_
  47.9 0.8 collective-permute-done.1.weight_ref
  48.7 0.7 multiply.3
  49.5 12.4 %all_to_all.28 = f32[8,128,128]{2,1,0:T(8,128)S(1)} all-to-all(f32[8,128,128]{2,1,0:T(8,128)S(1)} %bitcast.12), channel_id=1, replica_groups={{0,2,4,6,8,10,12,14},{16,18,20,22,24,26,28,30},{1,3,5,7,9,11,13,15},{17..., dimensions={0} | all-to-all | bytes 1048576 | tf_op jit(solution)/shard_map/all_to_all | solution.py:381
  61.9 0.9 %collective-permute-start.2 = (f32[128,128]{1,0:T(8,128)S(1)}, f32[128,128]{1,0:T(8,128)S(1)}, u32[]{:S(2)}, u32[]{:S(2)}) collective-permute-start(f32[128,128]{1,0:T(8,128)S(1)} %reduce_sum.9), channel_id=1, source_target_pairs={{0,16},{2,18},{4,20},{6,22},{8,24},{10,26},{12,28},{14,30},{16,0},... | collective-permute-start | bytes 196616 | tf_op jit(solution)/shard_map/ppermute | solution.py:418
  62.9 5.0 %collective-permute-done.2 = f32[128,128]{1,0:T(8,128)S(1)} collective-permute-done((f32[128,128]{1,0:T(8,128)S(1)}, f32[128,128]{1,0:T(8,128)S(1)}, u32[]{:S(2)}, u32[]{:S(2)}) %collective-permute-start.2) | collective-permute-done | bytes 65568 | tf_op jit(solution)/shard_map/ppermute | solution.py:418
  67.9 10.4 %all_to_all.29 = f32[8,128,128]{2,1,0:T(8,128)S(1)} all-to-all(f32[8,128,128]{2,1,0:T(8,128)S(1)} %reshape_tile.3), channel_id=1, replica_groups={{0,2,4,6,8,10,12,14},{16,18,20,22,24,26,28,30},{1,3,5,7,9,11,13,15},{17..., dimensions={0} | all-to-all | bytes 1048576 | tf_op jit(solution)/shard_map/all_to_all | solution.py:381
  78.3 0.3 row_gram.1.mine_ref
  78.7 0.1 collective-permute-start.3
  78.8 0.7 copy.5
  79.4 0.6 collective-permute-done.3.other_ref
  80.0 3.6 %finish.1 = f32[1024,128]{1,0:T(8,128)} custom-call(f32[1024,128]{1,0:T(8,128)S(1)} %bitcast.9, f32[128,128]{1,0:T(8,128)S(1)} %row_gram.1.mine_ref, f32[128,128]{1,0:T(8,128)S(1)} %collective-permute-done.3.other_ref), custom_call_target="tpu_custom_call" | custom-call | tf_op jit(solution)/shard_map/finish/pallas_call | solution.py:350
  (4 shorter events, 0.1 us)
Async XLA Ops:
  3.5 29.4 %copy-start = (f32[16,8]{0,1:T(8,128)S(1)}, f32[16,8]{0,1:T(8,128)}, u32[]{:S(2)}) copy-start(f32[16,8]{0,1:T(8,128)} %param.5) | copy-start | bytes 1540
  3.5 1.7 %collective-permute-start = (f32[16,2,8,256]{3,2,1,0:T(8,128)S(1)}, f32[16,2,8,256]{3,2,1,0:T(8,128)S(1)}, u32[]{:S(2)}, u32[]{:S(2)}) collective-permute-start(f32[16,2,8,256]{3,2,1,0:T(8,128)S(1)} %get-tuple-element.17), channel_id=1, source_target_pairs={{0,1},{1,0},{2,3},{3,2},{4,5},{5,4},{6,7},{7,6},{8,9},{9,8},{10,11... | collective-permute-start | bytes 786440 | tf_op jit(solution)/shard_map/ppermute | solution.py:397
  47.2 1.5 %collective-permute-start.1 = (f32[16,2,8,256]{3,2,1,0:T(8,128)S(1)}, f32[16,2,8,256]{3,2,1,0:T(8,128)S(1)}, u32[]{:S(2)}, u32[]{:S(2)}) collective-permute-start(f32[16,2,8,256]{3,2,1,0:T(8,128)S(1)} %bitcast.13), channel_id=1, source_target_pairs={{0,1},{1,0},{2,3},{3,2},{4,5},{5,4},{6,7},{7,6},{8,9},{9,8},{10,11... | collective-permute-start | bytes 786440 | tf_op jit(solution)/shard_map/ppermute | solution.py:414
  61.9 5.9 %collective-permute-start.2 = (f32[128,128]{1,0:T(8,128)S(1)}, f32[128,128]{1,0:T(8,128)S(1)}, u32[]{:S(2)}, u32[]{:S(2)}) collective-permute-start(f32[128,128]{1,0:T(8,128)S(1)} %reduce_sum.9), channel_id=1, source_target_pairs={{0,16},{2,18},{4,20},{6,22},{8,24},{10,26},{12,28},{14,30},{16,0},... | collective-permute-start | bytes 196616 | tf_op jit(solution)/shard_map/ppermute | solution.py:418
  78.7 1.3 %collective-permute-start.3 = (f32[128,128]{1,0:T(8,128)S(1)}, f32[128,128]{1,0:T(8,128)S(1)}, u32[]{:S(2)}, u32[]{:S(2)}) collective-permute-start(f32[128,128]{1,0:T(8,128)S(1)} %row_gram.1.mine_ref), channel_id=1, source_target_pairs={{0,1},{1,0},{2,3},{3,2},{4,5},{5,4},{6,7},{7,6},{8,9},{9,8},{10,11... | collective-permute-start | bytes 196616 | tf_op jit(solution)/shard_map/ppermute | solution.py:421
